TPU v7x, 32 devices: a whole 2x2x4 slice. The times are simulated.
32 devices in a mesh: member: 2 (over y), tx: 4 (over z), ty: 4 (over x, core).
Axes of the slice: x: 2, y: 2, z: 4, core: 2. Of those that a mesh axis runs over, the one named last changes fastest.
Arguments:
- tracers: float32 [80, 3, 128, 512], P('member', None, 'tx', 'ty'), parts along dimension 0, may hold values from 0.05 to 2
- velocity: float32 [2, 3, 128, 512], P(None, None, 'tx', 'ty'), may hold values from -0.4 to 0.4
- land_mask: int32 [3, 128, 512], P(None, 'tx', 'ty'), may hold values 0 or 1
- sunlight: float32 [128, 512], P('tx', 'ty'), may hold values from 0.3 to 3
- growth_max: float32 [52], P('member'), parts along dimension 0, may hold values from 0.2 to 1.5
- half_sat: float32 [8, 26], P('member'), parts along dimension 0, may hold values from 0.05 to 1
- light_half: float32 [52], P('member'), parts along dimension 0, may hold values from 0.1 to 1
- graze_max: float32 [20], P('member'), parts along dimension 0, may hold values from 0.2 to 1.5
- graze_half: float32 [20], P('member'), parts along dimension 0, may hold values from 0.2 to 2
- palatable: int32 [20, 26], P('member'), parts along dimension 0, may hold values 0 or 1
- stoichiometry: float32 [4], replicated, may hold values from 0.05 to 1
Outputs:
- updated: float32 [80, 3, 128, 512], P('member', None, 'tx', 'ty'), parts along dimension 0
There are 2 independent parts, one for each index of `member`. A program takes and returns all parts, laid end to end along the dimension named above; an argument that names none is the same for every part. Nothing has to cross between parts.
All inputs are finite; a program needn't handle non-finite values. No bound on the sum of `land_mask` on one device may be relied on, other than what follows from the above.
Results may differ from a plain program's by a relative error of at most 0.000064.
Values sent between devices are 32-bit elements; how exact they have to be, the bound alone decides.
A program may use at most 64 MiB of HBM per device.

v0:
```python
import functools

import jax
import jax.numpy as jnp
from jax import lax
from jax.experimental import pallas as pl
from jax.experimental.pallas import tpu as pltpu
from jax.sharding import PartitionSpec as P

NNUT = 4
plankton_mortality = 0.05
grazer_mortality = 0.3
assimilation = 0.3
attenuation = 0.4

ROWS = 8
LANES = 128
FIRST = 8
GROUP = 4
PER = LANES // GROUP
BATCH = 8
MESH = pl.DeviceIdType.MESH


def stencil_weights(here, after):
    hp, hm = jnp.maximum(here, 0.0), jnp.minimum(here, 0.0)
    ap, am = jnp.maximum(after, 0.0), jnp.minimum(after, 0.0)
    sixth = 1.0 / 6.0
    return (
        -sixth * hp,
        5.0 * sixth * hp + 2.0 * sixth * hm + sixth * ap,
        1.0 - 4.0 * sixth * hp - sixth * hm + sixth * ap + 4.0 * sixth * am,
        -sixth * hm - 2.0 * sixth * ap - 5.0 * sixth * am,
        sixth * am,
    )


def exchange_kernel(
    dims,
    tracers,
    velocity,
    land_mask,
    sunlight,
    *refs,
):
    sources, (swept, tend, halo), tables, buffers = refs[:7], refs[7:10], refs[10:17], refs[17:]
    growth_max, half_sat, light_half, graze_max, graze_half, palatable, stoichiometry = tables
    (
    pad,
    mask_buf,
    sun_buf,
    send_lo,
    send_hi,
    recv_lo,
    recv_hi,
    pack_in,
    pack_out,
    left_in,
    left_out,
    right_in,
    right_out,
    prey,
    load_sems,
    row_sems,
    col_sems,
    ) = buffers
    count, levels, along, nphy, nzoo = dims
    fields = count + 2
    tiles = along // ROWS
    inner = tiles - 2
    last = FIRST + along - ROWS
    tx_size, ty_size = lax.axis_size("tx"), lax.axis_size("ty")
    tx, ty = lax.axis_index("tx"), lax.axis_index("ty")
    up, down = lax.rem(tx + 1, tx_size), lax.rem(tx + tx_size - 1, tx_size)
    right, left = lax.rem(ty + 1, ty_size), lax.rem(ty + ty_size - 1, ty_size)

    def load(slot, src, dst):
        copy = pltpu.make_async_copy(src, dst, load_sems.at[slot])
        copy.start()
        return copy

    own = pl.ds(0, count)
    loads = [
        load(0, land_mask, mask_buf),
        load(1, velocity.at[0], pad.at[count, :, pl.ds(FIRST, along), :]),
        load(2, tracers.at[:, :, pl.ds(0, ROWS), :], pad.at[own, :, pl.ds(FIRST, ROWS), :]),
        load(3, tracers.at[:, :, pl.ds(along - ROWS, ROWS), :], pad.at[own, :, pl.ds(last, ROWS), :]),
        load(4, tracers.at[:, :, pl.ds(ROWS, along - 2 * ROWS), :],
             pad.at[own, :, pl.ds(FIRST + ROWS, along - 2 * ROWS), :]),
        load(5, velocity.at[1], pad.at[count + 2, :, pl.ds(FIRST, along), :]),
        load(6, sunlight, sun_buf),
    ]
    small = [load(7 + i, src, dst) for i, (src, dst) in enumerate(zip(sources, tables))]

    barrier = pltpu.get_barrier_semaphore()
    for target in ({"tx": up}, {"tx": down}, {"ty": right}, {"ty": left}):
        pl.semaphore_signal(barrier, inc=1, device_id=target, device_id_type=MESH)

    def to_float(z, carry):
        for k in range(nphy):
            prey[z, k] = palatable[z, k].astype(jnp.float32)
        return carry

    for copy in small:
        copy.wait()
    lax.fori_loop(0, nzoo, to_float, 0)

    loads[0].wait()
    pad[count + 1, :, FIRST:FIRST + along, :] = mask_buf[...].astype(jnp.float32)
    for slot in (1, 2, 3):
        loads[slot].wait()
    send_lo[...] = pad[0:fields, :, FIRST:FIRST + 2, :]
    send_hi[...] = pad[0:fields, :, FIRST + along - 2:FIRST + along, :]

    pl.semaphore_wait(barrier, 4)

    def remote(src, dst, sems, slot, target):
        return pltpu.make_async_remote_copy(
            src_ref=src, dst_ref=dst, send_sem=sems.at[slot, 0], recv_sem=sems.at[slot, 1],
            device_id=target, device_id_type=MESH,
        )

    to_down = remote(send_lo, recv_hi, row_sems, 0, {"tx": down})
    to_up = remote(send_hi, recv_lo, row_sems, 1, {"tx": up})
    to_down.start()
    to_up.start()
    for slot in (4, 5, 6):
        loads[slot].wait()

    lane_group = lax.broadcasted_iota(jnp.int32, (ROWS, LANES), 1) // GROUP

    def sweep(level, tile, pack, spot):
        base = FIRST + tile * ROWS

        def at(field, shift):
            return pad[field, level, pl.ds(base + shift, ROWS), :]

        wet = at(count + 1, 0)
        here = at(count, 0) * at(count + 1, -1) * wet
        after = at(count, 1) * wet * at(count + 1, 1)
        weights = stencil_weights(here, after)
        packed = [None] * (-(-fields // PER))
        for begin in range(0, fields, BATCH):
            batch = range(begin, min(begin + BATCH, fields))
            values = []
            for field in batch:
                if field < count:
                    value = at(field, -2) * weights[0]
                    for shift in range(-1, 3):
                        value = value + at(field, shift) * weights[shift + 2]
                elif field == count:
                    value = at(count + 2, 0)
                else:
                    value = wet
                values.append(value)
            for field, value in zip(batch, values):
                group, place = divmod(field, PER)
                turned = pltpu.roll(value, (GROUP * place + 2) % LANES, 1)
                if place == 0:
                    packed[group] = turned
                else:
                    packed[group] = jnp.where(lane_group == place, turned, packed[group])
            for field, value in zip(batch, values):
                swept[field, level, pl.ds(tile * ROWS, ROWS), :] = value
        for group, value in enumerate(packed):
            pack[level, spot, group] = value

    def sides(slot, pack, from_left, from_right):
        to_right = remote(pack, from_left, col_sems, slot, {"ty": right})
        to_left = remote(pack, from_right, col_sems, slot + 1, {"ty": left})
        return to_right, to_left

    has_left, has_right = ty > 0, ty < ty_size - 1

    def start(pair):
        pl.when(has_right)(pair[0].start)
        pl.when(has_left)(pair[1].start)

    def inner_level(level, carry):
        for tile in range(1, tiles - 1):
            sweep(level, tile, pack_in, tile - 1)
        return carry

    lax.fori_loop(0, levels, inner_level, 0)
    early = sides(0, pack_in, left_in, right_in)
    start(early)

    def ecology(level, carry):
        def field(index):
            return pad[index, level, pl.ds(FIRST, along), :]

        wet = field(count + 1)
        depth = jnp.full((along, LANES), -attenuation * (level.astype(jnp.float32) + 0.5), jnp.float32)
        light = sun_buf[...] * jnp.exp(depth)
        inverse = [1.0 / field(j) for j in range(NNUT)]
        recycled = jnp.zeros((along, LANES), jnp.float32)
        for k in range(nphy):
            phyto = field(NNUT + k)
            worst = inverse[0] * half_sat[0, k]
            for j in range(1, NNUT):
                worst = jnp.maximum(worst, inverse[j] * half_sat[j, k])
            growth = growth_max[k] * light * phyto / ((1.0 + worst) * (light + light_half[k]))
            loss = plankton_mortality * phyto
            change = growth - loss
            recycled = recycled - change
            tend[NNUT + k, level] = change
        available = [None] * nzoo
        for k in range(nphy):
            phyto = field(NNUT + k)
            for z in range(nzoo):
                term = prey[z, k] * phyto
                available[z] = term if k == 0 else available[z] + term
        rates = []
        for z in range(nzoo):
            zoo = field(NNUT + nphy + z)
            rate = graze_max[z] * zoo / (graze_half[z] + available[z])
            ingested = rate * available[z]
            loss = grazer_mortality * zoo * zoo
            tend[NNUT + nphy + z, level] = wet * (assimilation * ingested - loss)
            recycled = recycled + loss + (1.0 - assimilation) * ingested
            rates.append(rate)
        for k in range(nphy):
            eaten = prey[0, k] * rates[0]
            for z in range(1, nzoo):
                eaten = eaten + prey[z, k] * rates[z]
            tend[NNUT + k, level] = wet * (tend[NNUT + k, level] - field(NNUT + k) * eaten)
        recycled = wet * recycled
        for j in range(NNUT):
            tend[j, level] = stoichiometry[j] * recycled
        return carry

    lax.fori_loop(0, levels, ecology, 0)

    to_down.wait()
    to_up.wait()
    pad[0:fields, :, FIRST - 2:FIRST, :] = recv_lo[...]
    pad[0:fields, :, FIRST + along:FIRST + along + 2, :] = recv_hi[...]

    def outer_level(level, carry):
        sweep(level, 0, pack_out, 0)
        sweep(level, tiles - 1, pack_out, 1)
        return carry

    lax.fori_loop(0, levels, outer_level, 0)
    late = sides(2, pack_out, left_out, right_out)
    start(late)

    @pl.when(jnp.logical_not(has_left))
    def _():
        left_in[...] = jnp.zeros_like(left_in)
        left_out[...] = jnp.zeros_like(left_out)

    @pl.when(jnp.logical_not(has_right))
    def _():
        right_in[...] = jnp.zeros_like(right_in)
        right_out[...] = jnp.zeros_like(right_out)

    def finish(pair):
        @pl.when(has_right)
        def _():
            pair[0].wait_send()
            pair[1].wait_recv()

        @pl.when(has_left)
        def _():
            pair[1].wait_send()
            pair[0].wait_recv()

    finish(early)
    lane = lax.broadcasted_iota(jnp.int32, (ROWS, LANES), 1)
    from_left = (lane % GROUP) < 2

    def across_level(level, carry):
        for tile in range(1, tiles - 1):
            packs = [
                jnp.where(from_left, left_in[level, tile - 1, g], right_in[level, tile - 1, g])
                for g in range(halo.shape[2])
            ]
            across_tile(count, level, tile, packs, swept, tend, tend)
        return carry

    lax.fori_loop(0, levels, across_level, 0)
    finish(late)
    halo[...] = jnp.where(from_left, left_out[...], right_out[...])


def across_tile(count, level, tile, packs, swept, tend, result):
    lane = lax.broadcasted_iota(jnp.int32, (ROWS, LANES), 1)
    low, high = lane < 2, lane >= LANES - 2
    first, final = lane == 0, lane == LANES - 1
    rows = pl.ds(tile * ROWS, ROWS)

    def parts(field):
        group, place = divmod(field, PER)
        value = swept[field, level, rows, :]
        ends = pltpu.roll(packs[group], (-GROUP * place - 2) % LANES, 1)
        return value, ends

    def below(value, ends):
        return pltpu.roll(jnp.where(final, ends, value), 1, 1)

    def above(value, ends):
        return pltpu.roll(jnp.where(first, ends, value), LANES - 1, 1)

    flow, flow_ends = parts(count)
    wet, wet_ends = parts(count + 1)
    here = flow * below(wet, wet_ends) * wet
    after = above(flow, flow_ends) * wet * above(wet, wet_ends)
    weights = stencil_weights(here, after)
    for begin in range(0, count, BATCH):
        batch = range(begin, min(begin + BATCH, count))
        pairs = [parts(field) for field in batch]
        far_before = [pltpu.roll(jnp.where(high, e, v), 2, 1) for v, e in pairs]
        near_before = [below(v, e) for v, e in pairs]
        near_behind = [above(v, e) for v, e in pairs]
        far_behind = [pltpu.roll(jnp.where(low, e, v), LANES - 2, 1) for v, e in pairs]
        totals = []
        for i, field in enumerate(batch):
            total = tend[field, level, rows, :] + pairs[i][0] * weights[2]
            total = total + far_before[i] * weights[0] + near_before[i] * weights[1]
            total = total + near_behind[i] * weights[3] + far_behind[i] * weights[4]
            totals.append(total)
        for i, field in enumerate(batch):
            result[field, level, rows, :] = totals[i]


def across_kernel(dims, swept, tend, halo, updated, result, sems):
    count, levels, along = dims
    tiles = along // ROWS
    inner = pl.ds(ROWS, along - 2 * ROWS)
    copies = [pltpu.make_async_copy(tend.at[:, :, inner, :], updated.at[:, :, inner, :], sems.at[0])]
    copies[0].start()
    for spot, tile in enumerate((0, tiles - 1)):
        def step(level, carry):
            packs = [halo[level, spot, g] for g in range(halo.shape[2])]
            across_tile(count, level, tile, packs, swept, tend, result)
            return carry

        lax.fori_loop(0, levels, step, 0)
        rows = pl.ds(tile * ROWS, ROWS)
        copy = pltpu.make_async_copy(result.at[:, :, rows, :], updated.at[:, :, rows, :], sems.at[spot + 1])
        copy.start()
        copies.append(copy)
    for copy in copies:
        copy.wait()


def shards(
    tracers,
    velocity,
    land_mask,
    sunlight,
    growth_max,
    half_sat,
    light_half,
    graze_max,
    graze_half,
    palatable,
    stoichiometry,
):
    count, levels, along, across = tracers.shape
    assert across == LANES and along % ROWS == 0 and along >= 3 * ROWS
    nphy, nzoo = growth_max.shape[0], graze_max.shape[0]
    fields = count + 2
    groups = -(-fields // PER)
    tiles = along // ROWS
    f32 = jnp.float32
    any_space = pl.BlockSpec(memory_space=pl.ANY)
    hbm = pl.BlockSpec(memory_space=pltpu.HBM)
    vmem = pl.BlockSpec(memory_space=pltpu.VMEM)
    small = (growth_max, half_sat, light_half, graze_max, graze_half, palatable, stoichiometry)
    inner_shape = (levels, tiles - 2, groups, ROWS, LANES)
    outer_shape = (levels, 2, groups, ROWS, LANES)
    edge = (fields, levels, 2, LANES)
    swept, tend, halo = pl.pallas_call(
        functools.partial(exchange_kernel, (count, levels, along, nphy, nzoo)),
        out_shape=(
            jax.ShapeDtypeStruct((fields, levels, along, across), f32),
            jax.ShapeDtypeStruct(tracers.shape, f32),
            jax.ShapeDtypeStruct(outer_shape, f32),
        ),
        in_specs=[hbm] * 11,
        out_specs=(vmem, vmem, vmem),
        scratch_shapes=[pltpu.SMEM(x.shape, x.dtype) for x in small] + [
            pltpu.VMEM((count + 3, levels, FIRST + along + ROWS, LANES), f32),
            pltpu.VMEM(land_mask.shape, jnp.int32),
            pltpu.VMEM(sunlight.shape, f32),
            pltpu.VMEM(edge, f32),
            pltpu.VMEM(edge, f32),
            pltpu.VMEM(edge, f32),
            pltpu.VMEM(edge, f32),
            pltpu.VMEM(inner_shape, f32),
            pltpu.VMEM(outer_shape, f32),
            pltpu.VMEM(inner_shape, f32),
            pltpu.VMEM(outer_shape, f32),
            pltpu.VMEM(inner_shape, f32),
            pltpu.VMEM(outer_shape, f32),
            pltpu.SMEM(palatable.shape, f32),
            pltpu.SemaphoreType.DMA((14,)),
            pltpu.SemaphoreType.DMA((2, 2)),
            pltpu.SemaphoreType.DMA((4, 2)),
        ],
        compiler_params=pltpu.CompilerParams(
            collective_id=0, has_side_effects=True, vmem_limit_bytes=24 * 2**20
        ),
        name="exchange",
    )(*[
        pltpu.with_memory_space_constraint(x, pltpu.HBM)
        for x in (tracers, velocity, land_mask, sunlight) + small
    ])
    return pl.pallas_call(
        functools.partial(across_kernel, (count, levels, along)),
        out_shape=jax.ShapeDtypeStruct(tracers.shape, f32),
        in_specs=[vmem] * 3,
        out_specs=any_space,
        scratch_shapes=[pltpu.VMEM(tracers.shape, f32), pltpu.SemaphoreType.DMA((3,))],
        compiler_params=pltpu.CompilerParams(vmem_limit_bytes=24 * 2**20),
        name="across",
    )(swept, tend, halo)


def solution(mesh):
    return jax.shard_map(
        shards,
        mesh=mesh,
        in_specs=(
            P("member", None, "tx", "ty"),
            P(None, None, "tx", "ty"),
            P(None, "tx", "ty"),
            P("tx", "ty"),
            P("member"),
            P("member", None),
            P("member"),
            P("member"),
            P("member"),
            P("member", None),
            P(),
        ),
        out_specs=P("member", None, "tx", "ty"),
        check_vma=False,
    )
```

profile of v0, /device:TPU:0, one launch (start us, length us, event | category | flops | bytes accessed | tf_op | source)
XLA Modules:
  0.0 21.0 jit_solution(7860125425672112912)
XLA Ops:
  0.0 17.2 %exchange.1 = (f32[42,3,32,128]{3,2,1,0:T(8,128)S(1)}, f32[40,3,32,128]{3,2,1,0:T(8,128)S(1)}, f32[3,2,2,8,128]{4,3,2,1,0:T(8,128)S(1)}) custom-call(f32[40,3,32,128]{3,2,1,0:T(8,128)} %tracers.1, f32[2,3,32,128]{3,2,1,0:T(8,128)} %velocity.1, s32[3,32,128]{2,1,0:T(8,128)} %land_mask.1, f32[32,128]{1,0:T(8,128)} %sunlight.1, f32[26]{0:T(128)} %refs_0_.1, ...), custom_call_target="tpu_custom_call" | custom-call | tf_op jit(solution)/shard_map/exchange/pallas_call | solution.py:375
  17.2 3.8 %across.1 = f32[40,3,32,128]{3,2,1,0:T(8,128)} custom-call(f32[42,3,32,128]{3,2,1,0:T(8,128)S(1)} %get-tuple-element.8.swept, f32[40,3,32,128]{3,2,1,0:T(8,128)S(1)} %get-tuple-element.9.tend, f32[3,2,2,8,128]{4,3,2,1,0:T(8,128)S(1)} %get-tuple-element.10.halo), custom_call_target="tpu_custom_call" | custom-call | tf_op jit(solution)/shard_map/across/pallas_call | solution.py:411
where the time goes:
time: 21.2 us; the launch traced here: 21 us
  Pallas kernels  21 us (99%)
    pallas_call x1, Pallas kernels, shards(): pl.pallas_call(functools.partial(exchange_kernel, (count, levels, along,...  17.2 us
    pallas_call x1, Pallas kernels, shards(): pl.pallas_call(functools.partial(across_kernel, (count, levels, along)),...  3.78 us

commit v1 on v0

--- a/solution.py
+++ b/solution.py
@@ -122,8 +122,8 @@
 
     to_down = remote(send_lo, recv_hi, row_sems, 0, {"tx": down})
     to_up = remote(send_hi, recv_lo, row_sems, 1, {"tx": up})
+    to_up.start()
     to_down.start()
-    to_up.start()
     for slot in (4, 5, 6):
         loads[slot].wait()
 

time: 21.2 us -> 19.1 us (0.901)
  Pallas kernels: 21 us -> 19 us
    pallas_call x1, Pallas kernels: 17.2 us -> 15.2 us  [shards(): pl.pallas_call(functools.partial(exchange_kernel, (count, levels, along,...]
where the time goes in v1:
time: 19.1 us; the launch traced here: 19 us
  Pallas kernels  19 us (99%)
    pallas_call x1, Pallas kernels, shards(): pl.pallas_call(functools.partial(exchange_kernel, (count, levels, along,...  15.2 us
    pallas_call x1, Pallas kernels, shards(): pl.pallas_call(functools.partial(across_kernel, (count, levels, along)),...  3.78 us

profile of v1, /device:TPU:0, one launch (start us, length us, event | category | flops | bytes accessed | tf_op | source)
XLA Modules:
  0.0 19.0 jit_solution(7153511090867334829)
XLA Ops:
  0.0 15.2 %exchange.1 = (f32[42,3,32,128]{3,2,1,0:T(8,128)S(1)}, f32[40,3,32,128]{3,2,1,0:T(8,128)S(1)}, f32[3,2,2,8,128]{4,3,2,1,0:T(8,128)S(1)}) custom-call(f32[40,3,32,128]{3,2,1,0:T(8,128)} %tracers.1, f32[2,3,32,128]{3,2,1,0:T(8,128)} %velocity.1, s32[3,32,128]{2,1,0:T(8,128)} %land_mask.1, f32[32,128]{1,0:T(8,128)} %sunlight.1, f32[26]{0:T(128)} %refs_0_.1, ...), custom_call_target="tpu_custom_call" | custom-call | tf_op jit(solution)/shard_map/exchange/pallas_call | solution.py:375
  15.2 3.8 %across.1 = f32[40,3,32,128]{3,2,1,0:T(8,128)} custom-call(f32[42,3,32,128]{3,2,1,0:T(8,128)S(1)} %get-tuple-element.8.swept, f32[40,3,32,128]{3,2,1,0:T(8,128)S(1)} %get-tuple-element.9.tend, f32[3,2,2,8,128]{4,3,2,1,0:T(8,128)S(1)} %get-tuple-element.10.halo), custom_call_target="tpu_custom_call" | custom-call | tf_op jit(solution)/shard_map/across/pallas_call | solution.py:411

commit v2 on v1

v2 whole, which is shorter than its diff:
```python
import functools

import jax
import jax.numpy as jnp
from jax import lax
from jax.experimental import pallas as pl
from jax.experimental.pallas import tpu as pltpu
from jax.sharding import PartitionSpec as P

NNUT = 4
plankton_mortality = 0.05
grazer_mortality = 0.3
assimilation = 0.3
attenuation = 0.4

ROWS = 8
LANES = 128
FIRST = 8
GROUP = 4
PER = LANES // GROUP
BATCH = 20
MESH = pl.DeviceIdType.MESH


def stencil_weights(here, after):
    hp, hm = jnp.maximum(here, 0.0), jnp.minimum(here, 0.0)
    ap, am = jnp.maximum(after, 0.0), jnp.minimum(after, 0.0)
    sixth = 1.0 / 6.0
    return (
        -sixth * hp,
        5.0 * sixth * hp + 2.0 * sixth * hm + sixth * ap,
        1.0 - 4.0 * sixth * hp - sixth * hm + sixth * ap + 4.0 * sixth * am,
        -sixth * hm - 2.0 * sixth * ap - 5.0 * sixth * am,
        sixth * am,
    )


def place_of(field):
    return field // PER, PER - 1 - field % PER


def spread(value, lane, dims):
    return jnp.broadcast_to(value[:, lane:lane + 1], dims)


def packed_spread(value, field, quarter):
    start = GROUP * place_of(field)[1]
    parts = [spread(value, start + j, value.shape) for j in range(GROUP)]
    return jnp.where(quarter < 2, jnp.where(quarter == 0, parts[0], parts[1]),
                     jnp.where(quarter == 2, parts[2], parts[3]))


def exchange_kernel(dims, tracers, velocity, land_mask, sunlight, *refs):
    sources, outs, tables, buffers = refs[:7], refs[7:13], refs[13:20], refs[20:]
    result, own, far, base, along_w, across_w = outs
    growth_max, half_sat, light_half, graze_max, graze_half, palatable, stoichiometry = tables
    (
        pad, mask_buf, sun_buf, swept, tend, pack, left_in, right_in, qpad, halo_term, across_buf,
        strips, corner_out, corner_left, corner_right, halo_w, meta_out, meta_in, prey,
        load_sems, own_sems, send_sems, recv_sems,
    ) = buffers
    count, levels, along, nphy, nzoo, stride = dims
    tiles = along // ROWS
    flow_field, wet_field, cross_field = count, count + 1, count + 2
    groups = pack.shape[1]
    tx_size, ty_size = lax.axis_size("tx"), lax.axis_size("ty")
    tx, ty = lax.axis_index("tx"), lax.axis_index("ty")
    up, down = lax.rem(tx + 1, tx_size), lax.rem(tx + tx_size - 1, tx_size)
    right, left = lax.rem(ty + 1, ty_size), lax.rem(ty + ty_size - 1, ty_size)
    has_left, has_right = ty > 0, ty < ty_size - 1
    early = tx == 0

    barrier = pltpu.get_barrier_semaphore()

    def greet(**target):
        pl.semaphore_signal(barrier, inc=1, device_id=target, device_id_type=MESH)

    greet(tx=up)
    greet(tx=down)

    @pl.when(has_right)
    def _():
        greet(ty=right)
        greet(tx=up, ty=right)
        greet(tx=down, ty=right)

    @pl.when(has_left)
    def _():
        greet(ty=left)
        greet(tx=up, ty=left)
        greet(tx=down, ty=left)

    def gather():
        sides = has_left.astype(jnp.int32) + has_right.astype(jnp.int32)
        pl.semaphore_wait(barrier, 2 + 3 * sides)

    def own_copy(edge, level, k):
        row = k if edge == 0 else along - 4 + k
        return pltpu.make_async_copy(
            tracers.at[:, level, row, :], own.at[edge, level, k], own_sems.at[edge, level, k])

    def load(slot, src, dst):
        copy = pltpu.make_async_copy(src, dst, load_sems.at[slot])
        copy.start()
        return copy

    sent = [own_copy(1, level, k) for level in range(levels) for k in (2, 3)]
    sent_down = [own_copy(0, level, k) for level in range(levels) for k in (0, 1)]
    kept = [own_copy(edge, level, k + 2 * (1 - edge)) for edge in range(2) for level in range(levels) for k in range(2)]
    for copy in sent:
        copy.start()
    loads = [
        load(0, land_mask, mask_buf),
        load(1, velocity.at[0], pad.at[flow_field, :, pl.ds(FIRST, along), :]),
    ]
    for copy in sent_down:
        copy.start()
    loads += [
        load(2, tracers, pad.at[pl.ds(0, count), :, pl.ds(FIRST, along), :]),
        load(3, velocity.at[1], pad.at[cross_field, :, pl.ds(FIRST, along), :]),
        load(4, sunlight, sun_buf),
    ]
    small = [load(5 + i, src, dst) for i, (src, dst) in enumerate(zip(sources, tables))]
    for copy in kept:
        copy.start()

    def remote(slot, src, dst, **target):
        return pltpu.make_async_remote_copy(
            src_ref=src, dst_ref=dst, send_sem=send_sems.at[slot], recv_sem=recv_sems.at[slot],
            device_id=target, device_id_type=MESH)

    up_rows = remote(0, own.at[1, :, pl.ds(2, 2)], far.at[0], tx=up)
    down_rows = remote(1, own.at[0, :, pl.ds(0, 2)], far.at[1], tx=down)
    up_meta = remote(2, meta_out.at[1], meta_in.at[0], tx=up)
    down_meta = remote(3, meta_out.at[0], meta_in.at[1], tx=down)
    to_right = [
        remote(4, corner_out.at[1], corner_left.at[0], tx=up, ty=right),
        remote(5, corner_out.at[0], corner_left.at[1], tx=down, ty=right),
        remote(6, pack, left_in, ty=right),
    ]
    to_left = [
        remote(7, corner_out.at[1], corner_right.at[0], tx=up, ty=left),
        remote(8, corner_out.at[0], corner_right.at[1], tx=down, ty=left),
        remote(9, pack, right_in, ty=left),
    ]

    def first_sends():
        gather()
        up_rows.start()
        up_meta.start()
        down_meta.start()

    def last_sends():
        @pl.when(has_left)
        def _():
            for copy in to_left:
                copy.start()

        @pl.when(has_right)
        def _():
            for copy in to_right:
                copy.start()

        down_rows.start()

    loads[0].wait()
    pad[wet_field, :, FIRST:FIRST + along, :] = mask_buf[...].astype(jnp.float32)
    loads[1].wait()
    for edge, row in enumerate((FIRST, FIRST + along - 2)):
        meta_out[edge, 0] = pad[flow_field, :, row:row + 2, :]
        meta_out[edge, 1] = pad[wet_field, :, row:row + 2, :]
    for copy in sent:
        copy.wait()
    pl.when(jnp.logical_not(early))(first_sends)

    for copy in sent_down:
        copy.wait()
    for slot in (2, 3):
        loads[slot].wait()

    lane = lax.broadcasted_iota(jnp.int32, (ROWS, LANES), 1)
    lane_group = lane // GROUP
    quarter = lane % GROUP

    def pack_level(level, carry):
        for tile in (0, tiles - 1, *range(1, tiles - 1)):
            rows = pl.ds(FIRST + tile * ROWS, ROWS)
            packed = [None] * groups
            for field in range(count + 3):
                group, place = place_of(field)
                turned = pltpu.roll(pad[field, level, rows, :], (GROUP * place + 2) % LANES, 1)
                if packed[group] is None:
                    packed[group] = turned
                else:
                    packed[group] = jnp.where(lane_group == place, turned, packed[group])
            for group, value in enumerate(packed):
                pack[level, group, tile * ROWS:(tile + 1) * ROWS, :] = value
                for edge, edge_tile, row in ((0, 0, 0), (1, tiles - 1, ROWS - 2)):
                    if tile == edge_tile:
                        for r in range(2):
                            corner_out[edge, r, pl.ds(level * groups + group, 1), :] = value[row + r:row + r + 1, :]
        return carry

    lax.fori_loop(0, levels, pack_level, 0)
    pl.when(jnp.logical_not(early))(last_sends)

    def sweep_level(level, carry):
        for tile in range(tiles):
            start = FIRST + tile * ROWS

            def at(field, shift):
                return pad[field, level, pl.ds(start + shift, ROWS), :]

            wet = at(wet_field, 0)
            here = at(flow_field, 0) * at(wet_field, -1) * wet
            after = at(flow_field, 1) * wet * at(wet_field, 1)
            weights = stencil_weights(here, after)
            for begin in range(0, count, 8):
                batch = range(begin, min(begin + 8, count))
                values = []
                for field in batch:
                    value = at(field, -2) * weights[0]
                    for shift in range(-1, 3):
                        value = value + at(field, shift) * weights[shift + 2]
                    values.append(value)
                for field, value in zip(batch, values):
                    swept[field, level, tile * ROWS:(tile + 1) * ROWS, :] = value
        return carry

    lax.fori_loop(0, levels, sweep_level, 0)

    for copy in small:
        copy.wait()
    loads[4].wait()

    def to_float(z, carry):
        for k in range(nphy):
            prey[z, k] = palatable[z, k].astype(jnp.float32)
        return carry

    lax.fori_loop(0, nzoo, to_float, 0)

    def tend_rows(field, level, row=0, size=along):
        return pl.ds(pl.multiple_of(field * stride + level * along + row, ROWS), size)

    def ecology(level, carry):
        @pl.when(jnp.logical_and(early, level == levels - 1))
        def _():
            first_sends()
            last_sends()

        def field(index):
            return pad[index, level, pl.ds(FIRST, along), :]

        wet = field(wet_field)
        depth = jnp.full((along, LANES), -attenuation * (level.astype(jnp.float32) + 0.5), jnp.float32)
        light = sun_buf[...] * jnp.exp(depth)
        inverse = [1.0 / field(j) for j in range(NNUT)]
        recycled = jnp.zeros((along, LANES), jnp.float32)
        for k in range(nphy):
            phyto = field(NNUT + k)
            worst = inverse[0] * half_sat[0, k]
            for j in range(1, NNUT):
                worst = jnp.maximum(worst, inverse[j] * half_sat[j, k])
            growth = growth_max[k] * light * phyto / ((1.0 + worst) * (light + light_half[k]))
            loss = plankton_mortality * phyto
            change = growth - loss
            recycled = recycled - change
            tend[tend_rows(NNUT + k, level), :] = change
        available = [None] * nzoo
        for k in range(nphy):
            phyto = field(NNUT + k)
            for z in range(nzoo):
                term = prey[z, k] * phyto
                available[z] = term if k == 0 else available[z] + term
        rates = []
        for z in range(nzoo):
            zoo = field(NNUT + nphy + z)
            rate = graze_max[z] * zoo / (graze_half[z] + available[z])
            ingested = rate * available[z]
            loss = grazer_mortality * zoo * zoo
            tend[tend_rows(NNUT + nphy + z, level), :] = wet * (assimilation * ingested - loss)
            recycled = recycled + loss + (1.0 - assimilation) * ingested
            rates.append(rate)
        for k in range(nphy):
            eaten = prey[0, k] * rates[0]
            for z in range(1, nzoo):
                eaten = eaten + prey[z, k] * rates[z]
            rows = tend_rows(NNUT + k, level)
            tend[rows, :] = wet * (tend[rows, :] - field(NNUT + k) * eaten)
        recycled = wet * recycled
        for j in range(NNUT):
            tend[tend_rows(j, level), :] = stoichiometry[j] * recycled
        return carry

    lax.fori_loop(0, levels, ecology, 0)

    @pl.when(jnp.logical_not(has_left))
    def _():
        left_in[...] = jnp.zeros_like(left_in)
        corner_left[...] = jnp.zeros_like(corner_left)

    @pl.when(jnp.logical_not(has_right))
    def _():
        right_in[...] = jnp.zeros_like(right_in)
        corner_right[...] = jnp.zeros_like(corner_right)

    def finish(i):
        @pl.when(has_right)
        def _():
            to_right[i].wait_send()
            to_left[i].wait_recv()

        @pl.when(has_left)
        def _():
            to_left[i].wait_send()
            to_right[i].wait_recv()

    finish(2)
    full_lane = lax.broadcasted_iota(jnp.int32, (along, LANES), 1)
    full_quarter = full_lane % GROUP
    full = (along, LANES)
    ends = jnp.logical_or(lane < 2, lane >= LANES - 2)

    def join(from_left, from_right, which):
        return jnp.where(which < 2, pltpu.roll(from_right, LANES - 2, 1), pltpu.roll(from_left, 2, 1))

    def across_level(level, carry):
        middle = pl.ds(FIRST, along)
        joined = []
        for group in range(groups):
            value = join(left_in[level, group], right_in[level, group], full_quarter)
            qpad[group, middle, :] = value
            joined.append(value)
            for k in range(4):
                spot = pl.ds(level * groups + group, 1)
                strips[0, 2 + k, spot, :] = value[k:k + 1, :]
                strips[1, k, spot, :] = value[along - 4 + k:along - 3 + k, :]
        last = joined[groups - 1]
        qpad[groups, middle, :] = packed_spread(last, flow_field, full_quarter)
        qpad[groups + 1, middle, :] = packed_spread(last, wet_field, full_quarter)

        def q(index, shift):
            return qpad[index, pl.ds(FIRST + shift, along), :]

        wet = q(groups + 1, 0)
        here = q(groups, 0) * q(groups + 1, -1) * wet
        after = q(groups, 1) * wet * q(groups + 1, 1)
        weights = stencil_weights(here, after)

        wet_spot = GROUP * place_of(wet_field)[1]
        cross_spot = GROUP * place_of(cross_field)[1]
        cross, wet = pad[cross_field, level, middle, :], pad[wet_field, level, middle, :]
        first, final = full_lane == 0, full_lane == LANES - 1
        wet_below = jnp.where(first, spread(last, wet_spot + 3, full), pltpu.roll(wet, 1, 1))
        wet_above = jnp.where(final, spread(last, wet_spot, full), pltpu.roll(wet, LANES - 1, 1))
        cross_above = jnp.where(final, spread(last, cross_spot, full), pltpu.roll(cross, LANES - 1, 1))
        w = stencil_weights(cross * wet_below * wet, cross_above * wet * wet_above)
        near = jnp.where(full_quarter < 2,
                         jnp.where(full_quarter == 0, spread(w[4], LANES - 2, full), spread(w[4], LANES - 1, full)),
                         jnp.where(full_quarter == 2, spread(w[0], 0, full), spread(w[0], 1, full)))
        next_to = jnp.where(full_quarter == 1, spread(w[3], LANES - 1, full),
                            jnp.where(full_quarter == 2, spread(w[1], 0, full), 0.0))
        masked = (
            jnp.where(full_lane < 2, 0.0, w[0]),
            jnp.where(first, 0.0, w[1]),
            w[2],
            jnp.where(final, 0.0, w[3]),
            jnp.where(full_lane >= LANES - 2, 0.0, w[4]),
        )
        for i, value in enumerate(masked):
            across_buf[i] = value
        for edge, row in ((0, 0), (1, along - 2)):
            for r in range(2):
                for i, value in enumerate(masked):
                    across_w[edge, level, r, i:i + 1, :] = value[row + r:row + r + 1, :]
                for group in range(groups):
                    spot = pl.ds(level * groups + group, 1)
                    halo_w[0, edge, r, spot, :] = near[row + r:row + r + 1, :]
                    halo_w[1, edge, r, spot, :] = next_to[row + r:row + r + 1, :]
        for group in range(groups):
            total = q(group, -2) * weights[0]
            for shift in range(-1, 3):
                total = total + q(group, shift) * weights[shift + 2]
            beside = jnp.where(full_quarter == 1, pltpu.roll(total, 1, 1), pltpu.roll(total, LANES - 1, 1))
            halo_term[group] = near * total + next_to * beside

        for tile in range(tiles):
            rows = slice(tile * ROWS, (tile + 1) * ROWS)
            w = [across_buf[i, rows, :] for i in range(5)]
            terms = [halo_term[group, rows, :] for group in range(groups)]
            for begin in range(0, count, BATCH):
                batch = range(begin, min(begin + BATCH, count))
                totals = []
                for field in batch:
                    group, place = place_of(field)
                    value = swept[field, level, rows, :]
                    total = tend[tend_rows(field, level, tile * ROWS, ROWS), :] + value * w[2]
                    total = total + pltpu.roll(value, 2, 1) * w[0] + pltpu.roll(value, 1, 1) * w[1]
                    total = total + pltpu.roll(value, LANES - 1, 1) * w[3] + pltpu.roll(value, LANES - 2, 1) * w[4]
                    term = pltpu.roll(terms[group], (LANES - 2 - GROUP * place) % LANES, 1)
                    totals.append(total + jnp.where(ends, term, 0.0))
                for field, total in zip(batch, totals):
                    result[field, level, rows, :] = total
        return carry

    lax.fori_loop(0, levels, across_level, 0)

    for copy in kept:
        copy.wait()
    up_meta.wait()
    down_meta.wait()
    pad[wet_field, :, FIRST - 2:FIRST, :] = meta_in[0, 1]
    for i, index in enumerate((flow_field, wet_field)):
        pad[index, :, FIRST + along:FIRST + along + 2, :] = meta_in[1, i]
    for level in range(levels):
        for edge, tile, row in ((0, 0, 0), (1, tiles - 1, ROWS - 2)):
            start = FIRST + tile * ROWS

            def at(index, shift):
                return pad[index, level, start + shift:start + shift + ROWS, :]

            wet = at(wet_field, 0)
            weights = stencil_weights(at(flow_field, 0) * at(wet_field, -1) * wet,
                                      at(flow_field, 1) * wet * at(wet_field, 1))
            for r in range(2):
                for i, value in enumerate(weights):
                    along_w[edge, level, r, i:i + 1, :] = value[row + r:row + r + 1, :]

    finish(0)
    finish(1)
    odd = lax.broadcasted_iota(jnp.int32, (ROWS, LANES), 0) % groups == groups - 1
    for edge in range(2):
        for r in range(2):
            strips[edge, r + 4 * edge] = join(corner_left[edge, r], corner_right[edge, r], quarter)

        def both(value):
            return jnp.where(odd, value, pltpu.roll(value, ROWS - 1, 0))

        strip = [strips[edge, k] for k in range(6)]
        wets = {k: both(packed_spread(strip[k], wet_field, quarter)) for k in range(1, 5)}
        flows = {k: both(packed_spread(strip[k], flow_field, quarter)) for k in range(2, 5)}
        faces = {k: flows[k] * wets[k - 1] * wets[k] for k in range(2, 5)}
        for r in range(2):
            weights = stencil_weights(faces[r + 2], faces[r + 3])
            total = strip[r] * weights[0]
            for shift in range(1, 5):
                total = total + strip[r + shift] * weights[shift]
            beside = jnp.where(quarter == 1, pltpu.roll(total, 1, 1), pltpu.roll(total, LANES - 1, 1))
            term = halo_w[0, edge, r] * total + halo_w[1, edge, r] * beside
            row = r if edge == 0 else along - 2 + r
            for level in range(levels):
                for begin in range(0, count, ROWS):
                    group, inside = divmod(begin, PER)
                    line = jnp.broadcast_to(term[level * groups + group:level * groups + group + 1, :], (ROWS, LANES))
                    line = pltpu.roll(line, 2 + GROUP * inside, 1, stride=GROUP, stride_axis=0)
                    rows = pl.ds(begin * stride + level * along + row, ROWS, stride=stride)
                    base[edge, level, r, begin:begin + ROWS, :] = tend[rows, :] + jnp.where(ends, line, 0.0)

    up_rows.wait()
    down_rows.wait()


def across_kernel(dims, result, own, far, base, along_w, across_w, updated, rows_out, sems):
    count, levels, along = dims
    inner = pl.ds(2, along - 4)
    copies = [pltpu.make_async_copy(result.at[:, :, inner, :], updated.at[:, :, inner, :], sems.at[0])]
    copies[0].start()
    for edge in range(2):
        for level in range(levels):
            near = [own[edge, level, k] for k in range(4)]
            beyond = [far[edge, level, k] for k in range(2)]
            lines = beyond + near if edge == 0 else near + beyond
            for r in range(2):
                along_lines, across_lines = along_w[edge, level, r], across_w[edge, level, r]
                value = lines[r] * along_lines[0:1, :]
                for shift in range(1, 5):
                    value = value + lines[r + shift] * along_lines[shift:shift + 1, :]
                total = base[edge, level, r] + value * across_lines[2:3, :]
                total = total + pltpu.roll(value, 2, 1) * across_lines[0:1, :]
                total = total + pltpu.roll(value, 1, 1) * across_lines[1:2, :]
                total = total + pltpu.roll(value, LANES - 1, 1) * across_lines[3:4, :]
                total = total + pltpu.roll(value, LANES - 2, 1) * across_lines[4:5, :]
                rows_out[edge, level, r] = total
    for edge in range(2):
        for level in range(levels):
            for r in range(2):
                row = r if edge == 0 else along - 2 + r
                copy = pltpu.make_async_copy(
                    rows_out.at[edge, level, r], updated.at[:, level, row, :],
                    sems.at[1 + (edge * levels + level) * 2 + r])
                copy.start()
                copies.append(copy)
    for copy in copies:
        copy.wait()


def shards(
    tracers,
    velocity,
    land_mask,
    sunlight,
    growth_max,
    half_sat,
    light_half,
    graze_max,
    graze_half,
    palatable,
    stoichiometry,
):
    count, levels, along, across = tracers.shape
    nphy, nzoo = growth_max.shape[0], graze_max.shape[0]
    groups = -(-(count + 3) // PER)
    assert across == LANES and along % ROWS == 0 and along >= 2 * ROWS
    assert count % ROWS == 0 and groups == 2 and (count + 2) % PER >= 2 and levels * groups <= ROWS
    f32 = jnp.float32
    any_space = pl.BlockSpec(memory_space=pl.ANY)
    hbm = pl.BlockSpec(memory_space=pltpu.HBM)
    vmem = pl.BlockSpec(memory_space=pltpu.VMEM)
    small = (growth_max, half_sat, light_half, graze_max, graze_half, palatable, stoichiometry)
    stride = levels * along + ROWS
    line = (ROWS, LANES)
    columns = (levels, groups, along, LANES)
    outputs = [
        (count, levels, along, LANES),
        (2, levels, 4, count, LANES),
        (2, levels, 2, count, LANES),
        (2, levels, 2, count, LANES),
        (2, levels, 2) + line,
        (2, levels, 2) + line,
    ]
    prepared = pl.pallas_call(
        functools.partial(exchange_kernel, (count, levels, along, nphy, nzoo, stride)),
        out_shape=tuple(jax.ShapeDtypeStruct(shape, f32) for shape in outputs),
        in_specs=[hbm] * 11,
        out_specs=(vmem,) * len(outputs),
        scratch_shapes=[pltpu.SMEM(x.shape, x.dtype) for x in small] + [
            pltpu.VMEM((count + 3, levels, FIRST + along + ROWS, LANES), f32),
            pltpu.VMEM(land_mask.shape, jnp.int32),
            pltpu.VMEM(sunlight.shape, f32),
            pltpu.VMEM((count, levels, along, LANES), f32),
            pltpu.VMEM((count * stride, LANES), f32),
            pltpu.VMEM(columns, f32),
            pltpu.VMEM(columns, f32),
            pltpu.VMEM(columns, f32),
            pltpu.VMEM((groups + 2, FIRST + along + ROWS, LANES), f32),
            pltpu.VMEM((groups, along, LANES), f32),
            pltpu.VMEM((5, along, LANES), f32),
            pltpu.VMEM((2, 6) + line, f32),
            pltpu.VMEM((2, 2) + line, f32),
            pltpu.VMEM((2, 2) + line, f32),
            pltpu.VMEM((2, 2) + line, f32),
            pltpu.VMEM((2, 2, 2) + line, f32),
            pltpu.VMEM((2, 2, levels, 2, LANES), f32),
            pltpu.VMEM((2, 2, levels, 2, LANES), f32),
            pltpu.SMEM(palatable.shape, f32),
            pltpu.SemaphoreType.DMA((12,)),
            pltpu.SemaphoreType.DMA((2, levels, 4)),
            pltpu.SemaphoreType.DMA((10,)),
            pltpu.SemaphoreType.DMA((10,)),
        ],
        compiler_params=pltpu.CompilerParams(
            collective_id=0, has_side_effects=True, vmem_limit_bytes=32 * 2**20
        ),
        name="exchange",
    )(*[
        pltpu.with_memory_space_constraint(x, pltpu.HBM)
        for x in (tracers, velocity, land_mask, sunlight) + small
    ])
    return pl.pallas_call(
        functools.partial(across_kernel, (count, levels, along)),
        out_shape=jax.ShapeDtypeStruct(tracers.shape, f32),
        in_specs=[vmem] * len(outputs),
        out_specs=any_space,
        scratch_shapes=[
            pltpu.VMEM((2, levels, 2, count, LANES), f32),
            pltpu.SemaphoreType.DMA((1 + 4 * levels,)),
        ],
        compiler_params=pltpu.CompilerParams(vmem_limit_bytes=24 * 2**20),
        name="across",
    )(*prepared)


def solution(mesh):
    return jax.shard_map(
        shards,
        mesh=mesh,
        in_specs=(
            P("member", None, "tx", "ty"),
            P(None, None, "tx", "ty"),
            P(None, "tx", "ty"),
            P("tx", "ty"),
            P("member"),
            P("member", None),
            P("member"),
            P("member"),
            P("member"),
            P("member", None),
            P(),
        ),
        out_specs=P("member", None, "tx", "ty"),
        check_vma=False,
    )
```

time: 19.1 us -> 17.1 us (0.90)
  the two profiles are of different devices: /device:TPU:0 before, /device:TPU:1 now
where the time goes in v2:
time: 17.1 us; the launch traced here: 17 us
  Pallas kernels  17 us (99%)
    pallas_call x1, Pallas kernels, shards(): pl.pallas_call(functools.partial(exchange_kernel, (count, levels, along,...  15.3 us
    pallas_call x1, Pallas kernels, shards(): pl.pallas_call(functools.partial(across_kernel, (count, levels, along)),...  1.62 us

profile of v2, /device:TPU:1, one launch (start us, length us, event | category | flops | bytes accessed | tf_op | source)
XLA Modules:
  0.0 17.0 jit_solution(2362196238253785087)
XLA Ops:
  0.0 15.3 %exchange.1 = (f32[40,3,32,128]{3,2,1,0:T(8,128)S(1)}, f32[2,3,4,40,128]{4,3,2,1,0:T(8,128)S(1)}, f32[2,3,2,40,128]{4,3,2,1,0:T(8,128)S(1)}, f32[2,3,2,40,128]{4...) custom-call(f32[40,3,32,128]{3,2,1,0:T(8,128)} %tracers.1, ...), custom_call_target="tpu_custom_call" | custom-call | tf_op jit(solution)/shard_map/exchange/pallas_call | solution.py:532
  15.4 1.6 %across.1 = f32[40,3,32,128]{3,2,1,0:T(8,128)} custom-call(f32[40,3,32,128]{3,2,1,0:T(8,128)S(1)} %get-tuple-element.11.result, f32[2,3,4,40,128]{4,3,2,1,0:T(8,128)S(1)} %get-tuple-element.12.own, f32[2,3,2,40,128]{4,3,2,1,0:T(8,128)S(1)} %get-tuple-element.13.far, f32[2,3,2,40,128]{4,3,2,1,0:T(8,128)S(1)} %get-tuple-element.14.base, ...), custom_call_target="tpu_custom_call" | custom-call | tf_op jit(solution)/shard_map/across/pallas_call | solution.py:570

commit v3 on v2

--- a/solution.py
+++ b/solution.py
@@ -57,7 +57,7 @@
     (
         pad, mask_buf, sun_buf, swept, tend, pack, left_in, right_in, qpad, halo_term, across_buf,
         strips, corner_out, corner_left, corner_right, halo_w, meta_out, meta_in, prey,
-        load_sems, own_sems, send_sems, recv_sems,
+        load_sems, main_sems, own_sems, send_sems, recv_sems, ready_sems,
     ) = buffers
     count, levels, along, nphy, nzoo, stride = dims
     tiles = along // ROWS
@@ -68,31 +68,39 @@
     up, down = lax.rem(tx + 1, tx_size), lax.rem(tx + tx_size - 1, tx_size)
     right, left = lax.rem(ty + 1, ty_size), lax.rem(ty + ty_size - 1, ty_size)
     has_left, has_right = ty > 0, ty < ty_size - 1
-    early = tx == 0
+    at_first, at_last = tx == 0, tx == tx_size - 1
 
     barrier = pltpu.get_barrier_semaphore()
-
-    def greet(**target):
-        pl.semaphore_signal(barrier, inc=1, device_id=target, device_id_type=MESH)
-
-    greet(tx=up)
-    greet(tx=down)
+    TO_RIGHT, TO_UP, TO_UP_SIDES, TO_DOWN, TO_DOWN_SIDES = range(5)
+
+    def tell(sem, **target):
+        pl.semaphore_signal(sem, inc=1, device_id=target, device_id_type=MESH)
+
+    def tell_row(row, straight, aslant):
+        tell(straight, tx=row)
+
+        @pl.when(has_right)
+        def _():
+            tell(aslant, tx=row, ty=right)
+
+        @pl.when(has_left)
+        def _():
+            tell(aslant, tx=row, ty=left)
 
     @pl.when(has_right)
     def _():
-        greet(ty=right)
-        greet(tx=up, ty=right)
-        greet(tx=down, ty=right)
-
-    @pl.when(has_left)
-    def _():
-        greet(ty=left)
-        greet(tx=up, ty=left)
-        greet(tx=down, ty=left)
-
-    def gather():
-        sides = has_left.astype(jnp.int32) + has_right.astype(jnp.int32)
-        pl.semaphore_wait(barrier, 2 + 3 * sides)
+        tell(barrier, ty=right)
+
+    @pl.when(jnp.logical_not(at_last))
+    def _():
+        tell_row(up, barrier, barrier)
+
+    @pl.when(at_first)
+    def _():
+        tell_row(down, barrier, barrier)
+
+    lefts, rights = has_left.astype(jnp.int32), has_right.astype(jnp.int32)
+    sides = lefts + rights
 
     def own_copy(edge, level, k):
         row = k if edge == 0 else along - 4 + k
@@ -116,13 +124,37 @@
     for copy in sent_down:
         copy.start()
     loads += [
-        load(2, tracers, pad.at[pl.ds(0, count), :, pl.ds(FIRST, along), :]),
-        load(3, velocity.at[1], pad.at[cross_field, :, pl.ds(FIRST, along), :]),
-        load(4, sunlight, sun_buf),
+        load(2, velocity.at[1], pad.at[cross_field, :, pl.ds(FIRST, along), :]),
     ]
-    small = [load(5 + i, src, dst) for i, (src, dst) in enumerate(zip(sources, tables))]
+
+    def main(level):
+        return pltpu.make_async_copy(
+            tracers.at[:, level], pad.at[pl.ds(0, count), level, pl.ds(FIRST, along), :], main_sems.at[level])
+
+    for level in range(levels):
+        main(level).start()
+    loads.append(load(3, sunlight, sun_buf))
+    small = [load(4 + i, src, dst) for i, (src, dst) in enumerate(zip(sources, tables))]
     for copy in kept:
         copy.start()
+
+    earlier = lefts + jnp.where(at_first, 0, 1 + sides) + jnp.where(at_last, 1 + sides, 0)
+
+    @pl.when(earlier > 0)
+    def _():
+        pl.semaphore_wait(barrier, earlier)
+
+    @pl.when(has_left)
+    def _():
+        tell(ready_sems.at[TO_RIGHT], ty=left)
+
+    @pl.when(jnp.logical_not(at_first))
+    def _():
+        tell_row(down, ready_sems.at[TO_UP], ready_sems.at[TO_UP_SIDES])
+
+    @pl.when(at_last)
+    def _():
+        tell_row(up, ready_sems.at[TO_DOWN], ready_sems.at[TO_DOWN_SIDES])
 
     def remote(slot, src, dst, **target):
         return pltpu.make_async_remote_copy(
@@ -144,55 +176,70 @@
         remote(9, pack, right_in, ty=left),
     ]
 
-    def first_sends():
-        gather()
-        up_rows.start()
-        up_meta.start()
-        down_meta.start()
-
-    def last_sends():
-        @pl.when(has_left)
-        def _():
-            for copy in to_left:
+    def start(condition, copies):
+        @pl.when(condition)
+        def _():
+            for copy in copies:
                 copy.start()
 
-        @pl.when(has_right)
-        def _():
-            for copy in to_right:
-                copy.start()
-
-        down_rows.start()
-
-    loads[0].wait()
+    def start_sides(edge):
+        start(has_right, [to_right[1 - edge]])
+        start(has_left, [to_left[1 - edge]])
+
+    for copy in sent:
+        copy.wait()
+    start(at_last, [up_rows])
+    for copy in sent_down:
+        copy.wait()
+    start(jnp.logical_not(at_first), [down_rows])
+    for slot in range(3):
+        loads[slot].wait()
     pad[wet_field, :, FIRST:FIRST + along, :] = mask_buf[...].astype(jnp.float32)
-    loads[1].wait()
     for edge, row in enumerate((FIRST, FIRST + along - 2)):
         meta_out[edge, 0] = pad[flow_field, :, row:row + 2, :]
         meta_out[edge, 1] = pad[wet_field, :, row:row + 2, :]
-    for copy in sent:
-        copy.wait()
-    pl.when(jnp.logical_not(early))(first_sends)
-
-    for copy in sent_down:
-        copy.wait()
-    for slot in (2, 3):
-        loads[slot].wait()
 
     lane = lax.broadcasted_iota(jnp.int32, (ROWS, LANES), 1)
     lane_group = lane // GROUP
     quarter = lane % GROUP
 
-    def pack_level(level, carry):
+    def sweep_level(level, carry):
+        main(level).wait()
+
+        @pl.when(jnp.logical_and(jnp.logical_not(at_last), level == min(1, levels - 1)))
+        def _():
+            pl.semaphore_wait(ready_sems.at[TO_UP], 1)
+            up_meta.start()
+            up_rows.start()
+
         for tile in (0, tiles - 1, *range(1, tiles - 1)):
-            rows = pl.ds(FIRST + tile * ROWS, ROWS)
+            start_row = FIRST + tile * ROWS
+
+            def at(field, shift):
+                return pad[field, level, pl.ds(start_row + shift, ROWS), :]
+
+            wet = at(wet_field, 0)
+            here = at(flow_field, 0) * at(wet_field, -1) * wet
+            after = at(flow_field, 1) * wet * at(wet_field, 1)
+            weights = stencil_weights(here, after)
             packed = [None] * groups
-            for field in range(count + 3):
-                group, place = place_of(field)
-                turned = pltpu.roll(pad[field, level, rows, :], (GROUP * place + 2) % LANES, 1)
-                if packed[group] is None:
-                    packed[group] = turned
-                else:
-                    packed[group] = jnp.where(lane_group == place, turned, packed[group])
+            for begin in range(0, count + 3, 8):
+                batch = range(begin, min(begin + 8, count + 3))
+                values = []
+                for field in batch:
+                    if field < count:
+                        value = at(field, -2) * weights[0]
+                        for shift in range(-1, 3):
+                            value = value + at(field, shift) * weights[shift + 2]
+                        values.append(value)
+                    group, place = place_of(field)
+                    turned = pltpu.roll(at(field, 0), (GROUP * place + 2) % LANES, 1)
+                    if packed[group] is None:
+                        packed[group] = turned
+                    else:
+                        packed[group] = jnp.where(lane_group == place, turned, packed[group])
+                for field, value in zip(batch, values):
+                    swept[field, level, tile * ROWS:(tile + 1) * ROWS, :] = value
             for group, value in enumerate(packed):
                 pack[level, group, tile * ROWS:(tile + 1) * ROWS, :] = value
                 for edge, edge_tile, row in ((0, 0, 0), (1, tiles - 1, ROWS - 2)):
@@ -201,53 +248,44 @@
                             corner_out[edge, r, pl.ds(level * groups + group, 1), :] = value[row + r:row + r + 1, :]
         return carry
 
-    lax.fori_loop(0, levels, pack_level, 0)
-    pl.when(jnp.logical_not(early))(last_sends)
-
-    def sweep_level(level, carry):
-        for tile in range(tiles):
-            start = FIRST + tile * ROWS
-
-            def at(field, shift):
-                return pad[field, level, pl.ds(start + shift, ROWS), :]
-
-            wet = at(wet_field, 0)
-            here = at(flow_field, 0) * at(wet_field, -1) * wet
-            after = at(flow_field, 1) * wet * at(wet_field, 1)
-            weights = stencil_weights(here, after)
-            for begin in range(0, count, 8):
-                batch = range(begin, min(begin + 8, count))
-                values = []
-                for field in batch:
-                    value = at(field, -2) * weights[0]
-                    for shift in range(-1, 3):
-                        value = value + at(field, shift) * weights[shift + 2]
-                    values.append(value)
-                for field, value in zip(batch, values):
-                    swept[field, level, tile * ROWS:(tile + 1) * ROWS, :] = value
-        return carry
-
     lax.fori_loop(0, levels, sweep_level, 0)
+
+    @pl.when(at_last)
+    def _():
+        start_sides(1)
+        up_meta.start()
+
+    @pl.when(jnp.logical_not(at_first))
+    def _():
+        start_sides(0)
+        down_meta.start()
+
+    start(has_left, [to_left[2]])
+
+    @pl.when(has_right)
+    def _():
+        pl.semaphore_wait(ready_sems.at[TO_RIGHT], 1)
+        to_right[2].start()
+
 
     for copy in small:
         copy.wait()
-    loads[4].wait()
-
-    def to_float(z, carry):
+    loads[3].wait()
+    for z in range(nzoo):
         for k in range(nphy):
             prey[z, k] = palatable[z, k].astype(jnp.float32)
-        return carry
-
-    lax.fori_loop(0, nzoo, to_float, 0)
 
     def tend_rows(field, level, row=0, size=along):
         return pl.ds(pl.multiple_of(field * stride + level * along + row, ROWS), size)
 
     def ecology(level, carry):
-        @pl.when(jnp.logical_and(early, level == levels - 1))
-        def _():
-            first_sends()
-            last_sends()
+        @pl.when(jnp.logical_and(jnp.logical_not(at_last), level == min(1, levels - 1)))
+        def _():
+            @pl.when(sides > 0)
+            def _():
+                pl.semaphore_wait(ready_sems.at[TO_UP_SIDES], sides)
+
+            start_sides(1)
 
         def field(index):
             return pad[index, level, pl.ds(FIRST, along), :]
@@ -295,6 +333,13 @@
 
     lax.fori_loop(0, levels, ecology, 0)
 
+    @pl.when(at_first)
+    def _():
+        pl.semaphore_wait(ready_sems.at[TO_DOWN], 1)
+        down_meta.start()
+        down_rows.start()
+
+
     @pl.when(jnp.logical_not(has_left))
     def _():
         left_in[...] = jnp.zeros_like(left_in)
@@ -325,23 +370,23 @@
     def join(from_left, from_right, which):
         return jnp.where(which < 2, pltpu.roll(from_right, LANES - 2, 1), pltpu.roll(from_left, 2, 1))
 
-    def across_level(level, carry):
+    def halo_level(level):
         middle = pl.ds(FIRST, along)
         joined = []
         for group in range(groups):
             value = join(left_in[level, group], right_in[level, group], full_quarter)
-            qpad[group, middle, :] = value
+            qpad[level, group, middle, :] = value
             joined.append(value)
             for k in range(4):
-                spot = pl.ds(level * groups + group, 1)
+                spot = slice(level * groups + group, level * groups + group + 1)
                 strips[0, 2 + k, spot, :] = value[k:k + 1, :]
                 strips[1, k, spot, :] = value[along - 4 + k:along - 3 + k, :]
         last = joined[groups - 1]
-        qpad[groups, middle, :] = packed_spread(last, flow_field, full_quarter)
-        qpad[groups + 1, middle, :] = packed_spread(last, wet_field, full_quarter)
+        qpad[level, groups, middle, :] = packed_spread(last, flow_field, full_quarter)
+        qpad[level, groups + 1, middle, :] = packed_spread(last, wet_field, full_quarter)
 
         def q(index, shift):
-            return qpad[index, pl.ds(FIRST + shift, along), :]
+            return qpad[level, index, pl.ds(FIRST + shift, along), :]
 
         wet = q(groups + 1, 0)
         here = q(groups, 0) * q(groups + 1, -1) * wet
@@ -369,13 +414,13 @@
             jnp.where(full_lane >= LANES - 2, 0.0, w[4]),
         )
         for i, value in enumerate(masked):
-            across_buf[i] = value
+            across_buf[level, i] = value
         for edge, row in ((0, 0), (1, along - 2)):
             for r in range(2):
                 for i, value in enumerate(masked):
                     across_w[edge, level, r, i:i + 1, :] = value[row + r:row + r + 1, :]
                 for group in range(groups):
-                    spot = pl.ds(level * groups + group, 1)
+                    spot = slice(level * groups + group, level * groups + group + 1)
                     halo_w[0, edge, r, spot, :] = near[row + r:row + r + 1, :]
                     halo_w[1, edge, r, spot, :] = next_to[row + r:row + r + 1, :]
         for group in range(groups):
@@ -383,12 +428,24 @@
             for shift in range(-1, 3):
                 total = total + q(group, shift) * weights[shift + 2]
             beside = jnp.where(full_quarter == 1, pltpu.roll(total, 1, 1), pltpu.roll(total, LANES - 1, 1))
-            halo_term[group] = near * total + next_to * beside
+            halo_term[level, group] = near * total + next_to * beside
+
+    for level in range(levels):
+        halo_level(level)
+
+    def across_level(level, carry):
+        @pl.when(jnp.logical_and(at_first, level == min(1, levels - 1)))
+        def _():
+            @pl.when(sides > 0)
+            def _():
+                pl.semaphore_wait(ready_sems.at[TO_DOWN_SIDES], sides)
+
+            start_sides(0)
 
         for tile in range(tiles):
             rows = slice(tile * ROWS, (tile + 1) * ROWS)
-            w = [across_buf[i, rows, :] for i in range(5)]
-            terms = [halo_term[group, rows, :] for group in range(groups)]
+            w = [across_buf[level, i, rows, :] for i in range(5)]
+            terms = [halo_term[level, group, rows, :] for group in range(groups)]
             for begin in range(0, count, BATCH):
                 batch = range(begin, min(begin + BATCH, count))
                 totals = []
@@ -543,9 +600,9 @@
             pltpu.VMEM(columns, f32),
             pltpu.VMEM(columns, f32),
             pltpu.VMEM(columns, f32),
-            pltpu.VMEM((groups + 2, FIRST + along + ROWS, LANES), f32),
-            pltpu.VMEM((groups, along, LANES), f32),
-            pltpu.VMEM((5, along, LANES), f32),
+            pltpu.VMEM((levels, groups + 2, FIRST + along + ROWS, LANES), f32),
+            pltpu.VMEM((levels, groups, along, LANES), f32),
+            pltpu.VMEM((levels, 5, along, LANES), f32),
             pltpu.VMEM((2, 6) + line, f32),
             pltpu.VMEM((2, 2) + line, f32),
             pltpu.VMEM((2, 2) + line, f32),
@@ -554,10 +611,12 @@
             pltpu.VMEM((2, 2, levels, 2, LANES), f32),
             pltpu.VMEM((2, 2, levels, 2, LANES), f32),
             pltpu.SMEM(palatable.shape, f32),
-            pltpu.SemaphoreType.DMA((12,)),
+            pltpu.SemaphoreType.DMA((11,)),
+            pltpu.SemaphoreType.DMA((levels,)),
             pltpu.SemaphoreType.DMA((2, levels, 4)),
             pltpu.SemaphoreType.DMA((10,)),
             pltpu.SemaphoreType.DMA((10,)),
+            pltpu.SemaphoreType.REGULAR((5,)),
         ],
         compiler_params=pltpu.CompilerParams(
             collective_id=0, has_side_effects=True, vmem_limit_bytes=32 * 2**20

time: 17.1 us -> 15.8 us (0.924)
  the two profiles are of different devices: /device:TPU:1 before, /device:TPU:0 now
where the time goes in v3:
time: 15.8 us; the launch traced here: 15.7 us
  Pallas kernels  15.7 us (99%)
    pallas_call x1, Pallas kernels, shards(): pl.pallas_call(functools.partial(exchange_kernel, (count, levels, along,...  14.1 us
    pallas_call x1, Pallas kernels, shards(): pl.pallas_call(functools.partial(across_kernel, (count, levels, along)),...  1.62 us

profile of v3, /device:TPU:0, one launch (start us, length us, event | category | flops | bytes accessed | tf_op | source)
XLA Modules:
  0.0 15.7 jit_solution(9208809070840162606)
XLA Ops:
  0.0 14.1 %exchange.1 = (f32[40,3,32,128]{3,2,1,0:T(8,128)S(1)}, f32[2,3,4,40,128]{4,3,2,1,0:T(8,128)S(1)}, f32[2,3,2,40,128]{4,3,2,1,0:T(8,128)S(1)}, f32[2,3,2,40,128]{4...) custom-call(f32[40,3,32,128]{3,2,1,0:T(8,128)} %tracers.1, ...), custom_call_target="tpu_custom_call" | custom-call | tf_op jit(solution)/shard_map/exchange/pallas_call | solution.py:589
  14.1 1.6 %across.1 = f32[40,3,32,128]{3,2,1,0:T(8,128)} custom-call(f32[40,3,32,128]{3,2,1,0:T(8,128)S(1)} %get-tuple-element.11.result, f32[2,3,4,40,128]{4,3,2,1,0:T(8,128)S(1)} %get-tuple-element.12.own, f32[2,3,2,40,128]{4,3,2,1,0:T(8,128)S(1)} %get-tuple-element.13.far, f32[2,3,2,40,128]{4,3,2,1,0:T(8,128)S(1)} %get-tuple-element.14.base, ...), custom_call_target="tpu_custom_call" | custom-call | tf_op jit(solution)/shard_map/across/pallas_call | solution.py:629

commit v4 on v3

--- a/solution.py
+++ b/solution.py
@@ -50,14 +50,17 @@
                      jnp.where(quarter == 2, parts[2], parts[3]))
 
 
+def join(from_left, from_right, which):
+    return jnp.where(which < 2, pltpu.roll(from_right, LANES - 2, 1), pltpu.roll(from_left, 2, 1))
+
+
 def exchange_kernel(dims, tracers, velocity, land_mask, sunlight, *refs):
-    sources, outs, tables, buffers = refs[:7], refs[7:13], refs[13:20], refs[20:]
-    result, own, far, base, along_w, across_w = outs
+    sources, outs, tables, buffers = refs[:7], refs[7:17], refs[17:24], refs[24:]
+    result, own, far, tend, along_w, across_w, strips, corner_left, corner_right, halo_w = outs
     growth_max, half_sat, light_half, graze_max, graze_half, palatable, stoichiometry = tables
     (
-        pad, mask_buf, sun_buf, swept, tend, pack, left_in, right_in, qpad, halo_term, across_buf,
-        strips, corner_out, corner_left, corner_right, halo_w, meta_out, meta_in, prey,
-        load_sems, main_sems, own_sems, send_sems, recv_sems, ready_sems,
+        pad, mask_buf, sun_buf, swept, pack, left_in, right_in, qpad, halo_term, across_buf,
+        corner_out, meta_out, meta_in, prey, load_sems, main_sems, send_sems, recv_sems, ready_sems,
     ) = buffers
     count, levels, along, nphy, nzoo, stride = dims
     tiles = along // ROWS
@@ -69,6 +72,8 @@
     right, left = lax.rem(ty + 1, ty_size), lax.rem(ty + ty_size - 1, ty_size)
     has_left, has_right = ty > 0, ty < ty_size - 1
     at_first, at_last = tx == 0, tx == tx_size - 1
+    root = jnp.logical_and(at_first, jnp.logical_and(lax.axis_index("member") == 0, ty < 2))
+    others = jnp.logical_not(root)
 
     barrier = pltpu.get_barrier_semaphore()
     TO_RIGHT, TO_UP, TO_UP_SIDES, TO_DOWN, TO_DOWN_SIDES = range(5)
@@ -102,30 +107,29 @@
     lefts, rights = has_left.astype(jnp.int32), has_right.astype(jnp.int32)
     sides = lefts + rights
 
-    def own_copy(edge, level, k):
+    OWN_UP, OWN_DOWN, OWN_KEPT, PLANES, SUN, TABLE = range(6)
+
+    def own_copy(slot, edge, level, k):
         row = k if edge == 0 else along - 4 + k
-        return pltpu.make_async_copy(
-            tracers.at[:, level, row, :], own.at[edge, level, k], own_sems.at[edge, level, k])
-
-    def load(slot, src, dst):
-        copy = pltpu.make_async_copy(src, dst, load_sems.at[slot])
+        return pltpu.make_async_copy(tracers.at[:, level, row, :], own.at[edge, level, k], load_sems.at[slot])
+
+    def load(sem, src, dst):
+        copy = pltpu.make_async_copy(src, dst, sem)
         copy.start()
         return copy
 
-    sent = [own_copy(1, level, k) for level in range(levels) for k in (2, 3)]
-    sent_down = [own_copy(0, level, k) for level in range(levels) for k in (0, 1)]
-    kept = [own_copy(edge, level, k + 2 * (1 - edge)) for edge in range(2) for level in range(levels) for k in range(2)]
-    for copy in sent:
-        copy.start()
-    loads = [
-        load(0, land_mask, mask_buf),
-        load(1, velocity.at[0], pad.at[flow_field, :, pl.ds(FIRST, along), :]),
-    ]
-    for copy in sent_down:
-        copy.start()
-    loads += [
-        load(2, velocity.at[1], pad.at[cross_field, :, pl.ds(FIRST, along), :]),
-    ]
+    def await_load(slot, ref):
+        pltpu.make_async_copy(ref, ref, load_sems.at[slot]).wait()
+
+    for level in range(levels):
+        for k in (2, 3):
+            own_copy(OWN_UP, 1, level, k).start()
+    load(load_sems.at[PLANES], land_mask, mask_buf)
+    load(load_sems.at[PLANES], velocity.at[0], pad.at[flow_field, :, pl.ds(FIRST, along), :])
+    for level in range(levels):
+        for k in (0, 1):
+            own_copy(OWN_DOWN, 0, level, k).start()
+    load(load_sems.at[PLANES], velocity.at[1], pad.at[cross_field, :, pl.ds(FIRST, along), :])
 
     def main(level):
         return pltpu.make_async_copy(
@@ -133,10 +137,13 @@
 
     for level in range(levels):
         main(level).start()
-    loads.append(load(3, sunlight, sun_buf))
-    small = [load(4 + i, src, dst) for i, (src, dst) in enumerate(zip(sources, tables))]
-    for copy in kept:
-        copy.start()
+    sun = load(load_sems.at[SUN], sunlight, sun_buf)
+    table_sems = [load_sems.at[TABLE + i] for i in range(3)] + [send_sems.at[2 + i] for i in range(4)]
+    small = [load(sem, src, dst) for sem, src, dst in zip(table_sems, sources, tables)]
+    for level in range(levels):
+        for k in range(2):
+            own_copy(OWN_KEPT, 0, level, 2 + k).start()
+            own_copy(OWN_KEPT, 1, level, k).start()
 
     earlier = lefts + jnp.where(at_first, 0, 1 + sides) + jnp.where(at_last, 1 + sides, 0)
 
@@ -161,20 +168,25 @@
             src_ref=src, dst_ref=dst, send_sem=send_sems.at[slot], recv_sem=recv_sems.at[slot],
             device_id=target, device_id_type=MESH)
 
-    up_rows = remote(0, own.at[1, :, pl.ds(2, 2)], far.at[0], tx=up)
-    down_rows = remote(1, own.at[0, :, pl.ds(0, 2)], far.at[1], tx=down)
-    up_meta = remote(2, meta_out.at[1], meta_in.at[0], tx=up)
-    down_meta = remote(3, meta_out.at[0], meta_in.at[1], tx=down)
+    ROW, META, RIGHT_CORNERS, RIGHT_COLUMNS, LEFT_CORNERS, LEFT_COLUMNS = range(6)
+    up_rows = remote(ROW, own.at[1, :, pl.ds(2, 2)], far.at[0], tx=up)
+    down_rows = remote(ROW, own.at[0, :, pl.ds(0, 2)], far.at[1], tx=down)
+    up_meta = remote(META, meta_out.at[1], meta_in.at[0], tx=up)
+    down_meta = remote(META, meta_out.at[0], meta_in.at[1], tx=down)
     to_right = [
-        remote(4, corner_out.at[1], corner_left.at[0], tx=up, ty=right),
-        remote(5, corner_out.at[0], corner_left.at[1], tx=down, ty=right),
-        remote(6, pack, left_in, ty=right),
+        remote(RIGHT_CORNERS, corner_out.at[1], corner_left.at[0], tx=up, ty=right),
+        remote(RIGHT_CORNERS, corner_out.at[0], corner_left.at[1], tx=down, ty=right),
+        remote(RIGHT_COLUMNS, pack, left_in, ty=right),
     ]
     to_left = [
-        remote(7, corner_out.at[1], corner_right.at[0], tx=up, ty=left),
-        remote(8, corner_out.at[0], corner_right.at[1], tx=down, ty=left),
-        remote(9, pack, right_in, ty=left),
+        remote(LEFT_CORNERS, corner_out.at[1], corner_right.at[0], tx=up, ty=left),
+        remote(LEFT_CORNERS, corner_out.at[0], corner_right.at[1], tx=down, ty=left),
+        remote(LEFT_COLUMNS, pack, right_in, ty=left),
     ]
+    both_rows = remote(ROW, far, far, tx=up)
+    both_metas = remote(META, meta_in, meta_in, tx=up)
+    right_corners = remote(RIGHT_CORNERS, corner_left, corner_left, tx=up)
+    left_corners = remote(LEFT_CORNERS, corner_right, corner_right, tx=up)
 
     def start(condition, copies):
         @pl.when(condition)
@@ -186,18 +198,18 @@
         start(has_right, [to_right[1 - edge]])
         start(has_left, [to_left[1 - edge]])
 
-    for copy in sent:
-        copy.wait()
-    start(at_last, [up_rows])
-    for copy in sent_down:
-        copy.wait()
-    start(jnp.logical_not(at_first), [down_rows])
-    for slot in range(3):
-        loads[slot].wait()
+    await_load(OWN_UP, own.at[1, :, pl.ds(2, 2)])
+    odd_core = lax.rem(ty, 2) == 1
+    start(jnp.logical_and(at_last, jnp.logical_not(odd_core)), [up_rows])
+    await_load(OWN_DOWN, own.at[0, :, pl.ds(0, 2)])
+    await_load(PLANES, pad.at[pl.ds(count, 3), :, pl.ds(FIRST, along), :])
     pad[wet_field, :, FIRST:FIRST + along, :] = mask_buf[...].astype(jnp.float32)
     for edge, row in enumerate((FIRST, FIRST + along - 2)):
         meta_out[edge, 0] = pad[flow_field, :, row:row + 2, :]
         meta_out[edge, 1] = pad[wet_field, :, row:row + 2, :]
+    start(at_last, [up_meta, down_meta])
+    middle = jnp.logical_not(jnp.logical_or(at_first, at_last))
+    start(middle, [down_meta, down_rows])
 
     lane = lax.broadcasted_iota(jnp.int32, (ROWS, LANES), 1)
     lane_group = lane // GROUP
@@ -205,12 +217,6 @@
 
     def sweep_level(level, carry):
         main(level).wait()
-
-        @pl.when(jnp.logical_and(jnp.logical_not(at_last), level == min(1, levels - 1)))
-        def _():
-            pl.semaphore_wait(ready_sems.at[TO_UP], 1)
-            up_meta.start()
-            up_rows.start()
 
         for tile in (0, tiles - 1, *range(1, tiles - 1)):
             start_row = FIRST + tile * ROWS
@@ -249,18 +255,26 @@
         return carry
 
     lax.fori_loop(0, levels, sweep_level, 0)
-
-    @pl.when(at_last)
-    def _():
-        start_sides(1)
+    for copy in small:
+        copy.wait()
+    sun.wait()
+
+    def send_up():
+        pl.semaphore_wait(ready_sems.at[TO_UP], 1)
         up_meta.start()
-
-    @pl.when(jnp.logical_not(at_first))
-    def _():
-        start_sides(0)
+        up_rows.start()
+
+    def send_down():
+        pl.semaphore_wait(ready_sems.at[TO_DOWN], 1)
         down_meta.start()
-
+        down_rows.start()
+
+    pl.when(at_last)(lambda: start_sides(1))
+    pl.when(jnp.logical_not(at_first))(lambda: start_sides(0))
     start(has_left, [to_left[2]])
+    start(jnp.logical_and(at_last, odd_core), [up_rows])
+    start(at_last, [down_rows])
+    pl.when(jnp.logical_and(others, jnp.logical_not(at_last)))(send_up)
 
     @pl.when(has_right)
     def _():
@@ -268,9 +282,6 @@
         to_right[2].start()
 
 
-    for copy in small:
-        copy.wait()
-    loads[3].wait()
     for z in range(nzoo):
         for k in range(nphy):
             prey[z, k] = palatable[z, k].astype(jnp.float32)
@@ -279,7 +290,11 @@
         return pl.ds(pl.multiple_of(field * stride + level * along + row, ROWS), size)
 
     def ecology(level, carry):
-        @pl.when(jnp.logical_and(jnp.logical_not(at_last), level == min(1, levels - 1)))
+        second = level == min(1, levels - 1)
+        pl.when(jnp.logical_and(root, second))(send_up)
+        pl.when(jnp.logical_and(jnp.logical_and(at_first, others), second))(send_down)
+
+        @pl.when(jnp.logical_and(jnp.logical_not(at_last), second))
         def _():
             @pl.when(sides > 0)
             def _():
@@ -332,12 +347,7 @@
         return carry
 
     lax.fori_loop(0, levels, ecology, 0)
-
-    @pl.when(at_first)
-    def _():
-        pl.semaphore_wait(ready_sems.at[TO_DOWN], 1)
-        down_meta.start()
-        down_rows.start()
+    pl.when(root)(send_down)
 
 
     @pl.when(jnp.logical_not(has_left))
@@ -350,25 +360,22 @@
         right_in[...] = jnp.zeros_like(right_in)
         corner_right[...] = jnp.zeros_like(corner_right)
 
-    def finish(i):
+    def finish(to_right, to_left):
         @pl.when(has_right)
         def _():
-            to_right[i].wait_send()
-            to_left[i].wait_recv()
+            to_right.wait_send()
+            to_left.wait_recv()
 
         @pl.when(has_left)
         def _():
-            to_left[i].wait_send()
-            to_right[i].wait_recv()
-
-    finish(2)
+            to_left.wait_send()
+            to_right.wait_recv()
+
+    finish(to_right[2], to_left[2])
     full_lane = lax.broadcasted_iota(jnp.int32, (along, LANES), 1)
     full_quarter = full_lane % GROUP
     full = (along, LANES)
     ends = jnp.logical_or(lane < 2, lane >= LANES - 2)
-
-    def join(from_left, from_right, which):
-        return jnp.where(which < 2, pltpu.roll(from_right, LANES - 2, 1), pltpu.roll(from_left, 2, 1))
 
     def halo_level(level):
         middle = pl.ds(FIRST, along)
@@ -463,10 +470,8 @@
 
     lax.fori_loop(0, levels, across_level, 0)
 
-    for copy in kept:
-        copy.wait()
-    up_meta.wait()
-    down_meta.wait()
+    await_load(OWN_KEPT, far)
+    both_metas.wait()
     pad[wet_field, :, FIRST - 2:FIRST, :] = meta_in[0, 1]
     for i, index in enumerate((flow_field, wet_field)):
         pad[index, :, FIRST + along:FIRST + along + 2, :] = meta_in[1, i]
@@ -484,17 +489,34 @@
                 for i, value in enumerate(weights):
                     along_w[edge, level, r, i:i + 1, :] = value[row + r:row + r + 1, :]
 
-    finish(0)
-    finish(1)
+    finish(right_corners, left_corners)
+    both_rows.wait()
+
+
+def across_kernel(dims, result, own, far, tend, along_w, across_w, strips, corner_left, corner_right, halo_w,
+                  updated, rows_out, sems):
+    count, levels, along, stride = dims
+    groups = -(-(count + 3) // PER)
+    flow_field, wet_field = count, count + 1
+    inner = pl.ds(2, along - 4)
+    whole = pltpu.make_async_copy(result.at[:, :, inner, :], updated.at[:, :, inner, :], sems.at[0])
+    whole.start()
+
+    lane = lax.broadcasted_iota(jnp.int32, (ROWS, LANES), 1)
+    quarter = lane % GROUP
+    ends = jnp.logical_or(lane < 2, lane >= LANES - 2)
     odd = lax.broadcasted_iota(jnp.int32, (ROWS, LANES), 0) % groups == groups - 1
+
+    def both(value):
+        return jnp.where(odd, value, pltpu.roll(value, ROWS - 1, 0))
+
+    terms = {}
     for edge in range(2):
-        for r in range(2):
-            strips[edge, r + 4 * edge] = join(corner_left[edge, r], corner_right[edge, r], quarter)
-
-        def both(value):
-            return jnp.where(odd, value, pltpu.roll(value, ROWS - 1, 0))
-
-        strip = [strips[edge, k] for k in range(6)]
+        strip = [
+            join(corner_left[edge, k - 4 * edge], corner_right[edge, k - 4 * edge], quarter)
+            if k - 4 * edge in (0, 1) else strips[edge, k]
+            for k in range(6)
+        ]
         wets = {k: both(packed_spread(strip[k], wet_field, quarter)) for k in range(1, 5)}
         flows = {k: both(packed_spread(strip[k], flow_field, quarter)) for k in range(2, 5)}
         faces = {k: flows[k] * wets[k - 1] * wets[k] for k in range(2, 5)}
@@ -504,52 +526,36 @@
             for shift in range(1, 5):
                 total = total + strip[r + shift] * weights[shift]
             beside = jnp.where(quarter == 1, pltpu.roll(total, 1, 1), pltpu.roll(total, LANES - 1, 1))
-            term = halo_w[0, edge, r] * total + halo_w[1, edge, r] * beside
-            row = r if edge == 0 else along - 2 + r
-            for level in range(levels):
-                for begin in range(0, count, ROWS):
-                    group, inside = divmod(begin, PER)
-                    line = jnp.broadcast_to(term[level * groups + group:level * groups + group + 1, :], (ROWS, LANES))
-                    line = pltpu.roll(line, 2 + GROUP * inside, 1, stride=GROUP, stride_axis=0)
-                    rows = pl.ds(begin * stride + level * along + row, ROWS, stride=stride)
-                    base[edge, level, r, begin:begin + ROWS, :] = tend[rows, :] + jnp.where(ends, line, 0.0)
-
-    up_rows.wait()
-    down_rows.wait()
-
-
-def across_kernel(dims, result, own, far, base, along_w, across_w, updated, rows_out, sems):
-    count, levels, along = dims
-    inner = pl.ds(2, along - 4)
-    copies = [pltpu.make_async_copy(result.at[:, :, inner, :], updated.at[:, :, inner, :], sems.at[0])]
-    copies[0].start()
+            terms[edge, r] = halo_w[0, edge, r] * total + halo_w[1, edge, r] * beside
+
     for edge in range(2):
         for level in range(levels):
             near = [own[edge, level, k] for k in range(4)]
             beyond = [far[edge, level, k] for k in range(2)]
             lines = beyond + near if edge == 0 else near + beyond
             for r in range(2):
+                row = r if edge == 0 else along - 2 + r
                 along_lines, across_lines = along_w[edge, level, r], across_w[edge, level, r]
                 value = lines[r] * along_lines[0:1, :]
                 for shift in range(1, 5):
                     value = value + lines[r + shift] * along_lines[shift:shift + 1, :]
-                total = base[edge, level, r] + value * across_lines[2:3, :]
+                total = value * across_lines[2:3, :]
                 total = total + pltpu.roll(value, 2, 1) * across_lines[0:1, :]
                 total = total + pltpu.roll(value, 1, 1) * across_lines[1:2, :]
                 total = total + pltpu.roll(value, LANES - 1, 1) * across_lines[3:4, :]
                 total = total + pltpu.roll(value, LANES - 2, 1) * across_lines[4:5, :]
-                rows_out[edge, level, r] = total
-    for edge in range(2):
-        for level in range(levels):
-            for r in range(2):
-                row = r if edge == 0 else along - 2 + r
-                copy = pltpu.make_async_copy(
-                    rows_out.at[edge, level, r], updated.at[:, level, row, :],
-                    sems.at[1 + (edge * levels + level) * 2 + r])
-                copy.start()
-                copies.append(copy)
-    for copy in copies:
-        copy.wait()
+                for begin in range(0, count, ROWS):
+                    group, inside = divmod(begin, PER)
+                    spot = level * groups + group
+                    line = jnp.broadcast_to(terms[edge, r][spot:spot + 1, :], (ROWS, LANES))
+                    line = pltpu.roll(line, 2 + GROUP * inside, 1, stride=GROUP, stride_axis=0)
+                    rows = pl.ds(begin * stride + level * along + row, ROWS, stride=stride)
+                    rows_out[edge, level, r, begin:begin + ROWS, :] = (
+                        total[begin:begin + ROWS, :] + tend[rows, :] + jnp.where(ends, line, 0.0))
+                pltpu.make_async_copy(
+                    rows_out.at[edge, level, r], updated.at[:, level, row, :], sems.at[1]).start()
+    whole.wait()
+    pltpu.make_async_copy(rows_out, rows_out, sems.at[1]).wait()
 
 
 def shards(
@@ -582,9 +588,13 @@
         (count, levels, along, LANES),
         (2, levels, 4, count, LANES),
         (2, levels, 2, count, LANES),
-        (2, levels, 2, count, LANES),
+        (count * stride, LANES),
         (2, levels, 2) + line,
         (2, levels, 2) + line,
+        (2, 6) + line,
+        (2, 2) + line,
+        (2, 2) + line,
+        (2, 2, 2) + line,
     ]
     prepared = pl.pallas_call(
         functools.partial(exchange_kernel, (count, levels, along, nphy, nzoo, stride)),
@@ -596,26 +606,20 @@
             pltpu.VMEM(land_mask.shape, jnp.int32),
             pltpu.VMEM(sunlight.shape, f32),
             pltpu.VMEM((count, levels, along, LANES), f32),
-            pltpu.VMEM((count * stride, LANES), f32),
             pltpu.VMEM(columns, f32),
             pltpu.VMEM(columns, f32),
             pltpu.VMEM(columns, f32),
             pltpu.VMEM((levels, groups + 2, FIRST + along + ROWS, LANES), f32),
             pltpu.VMEM((levels, groups, along, LANES), f32),
             pltpu.VMEM((levels, 5, along, LANES), f32),
-            pltpu.VMEM((2, 6) + line, f32),
             pltpu.VMEM((2, 2) + line, f32),
-            pltpu.VMEM((2, 2) + line, f32),
-            pltpu.VMEM((2, 2) + line, f32),
-            pltpu.VMEM((2, 2, 2) + line, f32),
             pltpu.VMEM((2, 2, levels, 2, LANES), f32),
             pltpu.VMEM((2, 2, levels, 2, LANES), f32),
             pltpu.SMEM(palatable.shape, f32),
-            pltpu.SemaphoreType.DMA((11,)),
+            pltpu.SemaphoreType.DMA((8,)),
             pltpu.SemaphoreType.DMA((levels,)),
-            pltpu.SemaphoreType.DMA((2, levels, 4)),
-            pltpu.SemaphoreType.DMA((10,)),
-            pltpu.SemaphoreType.DMA((10,)),
+            pltpu.SemaphoreType.DMA((6,)),
+            pltpu.SemaphoreType.DMA((6,)),
             pltpu.SemaphoreType.REGULAR((5,)),
         ],
         compiler_params=pltpu.CompilerParams(
@@ -627,13 +631,13 @@
         for x in (tracers, velocity, land_mask, sunlight) + small
     ])
     return pl.pallas_call(
-        functools.partial(across_kernel, (count, levels, along)),
+        functools.partial(across_kernel, (count, levels, along, stride)),
         out_shape=jax.ShapeDtypeStruct(tracers.shape, f32),
         in_specs=[vmem] * len(outputs),
         out_specs=any_space,
         scratch_shapes=[
             pltpu.VMEM((2, levels, 2, count, LANES), f32),
-            pltpu.SemaphoreType.DMA((1 + 4 * levels,)),
+            pltpu.SemaphoreType.DMA((2,)),
         ],
         compiler_params=pltpu.CompilerParams(vmem_limit_bytes=24 * 2**20),
         name="across",

time: 15.8 us -> 13.2 us (0.84)
  the two profiles are of different devices: /device:TPU:0 before, /device:TPU:1 now
where the time goes in v4:
time: 13.2 us; the launch traced here: 13 us
  Pallas kernels  13 us (98%)
    pallas_call x1, Pallas kernels, shards(): pl.pallas_call(functools.partial(exchange_kernel, (count, levels, along,...  11.5 us
    pallas_call x1, Pallas kernels, shards(): pl.pallas_call(functools.partial(across_kernel, (count, levels, along, st...  1.54 us

profile of v4, /device:TPU:1, one launch (start us, length us, event | category | flops | bytes accessed | tf_op | source)
XLA Modules:
  0.0 13.0 jit_solution(3356238484235847248)
XLA Ops:
  0.0 11.5 %exchange.1 = (f32[40,3,32,128]{3,2,1,0:T(8,128)S(1)}, f32[2,3,4,40,128]{4,3,2,1,0:T(8,128)S(1)}, f32[2,3,2,40,128]{4,3,2,1,0:T(8,128)S(1)}, f32[4160,128]{1,0:T...) custom-call(f32[40,3,32,128]{3,2,1,0:T(8,128)} %tracers.1, ...), custom_call_target="tpu_custom_call" | custom-call | tf_op jit(solution)/shard_map/exchange/pallas_call | solution.py:599
  11.5 1.5 %across.1 = f32[40,3,32,128]{3,2,1,0:T(8,128)} custom-call(f32[40,3,32,128]{3,2,1,0:T(8,128)S(1)} %get-tuple-element.15.result, f32[2,3,4,40,128]{4,3,2,1,0:T(8,128)S(1)} %get-tuple-element.16.own, f32[2,3,2,40,128]{4,3,2,1,0:T(8,128)S(1)} %get-tuple-element.17.far, f32[4160,128]{1,0:T(8,128)S(1)} %get-tuple-element.18.tend, ...), custom_call_target="tpu_custom_call" | custom-call | tf_op jit(solution)/shard_map/across/pallas_call | solution.py:633

commit v5 on v4

--- a/solution.py
+++ b/solution.py
@@ -18,7 +18,8 @@
 FIRST = 8
 GROUP = 4
 PER = LANES // GROUP
-BATCH = 20
+BATCH = 8
+HALF = ROWS // 2
 MESH = pl.DeviceIdType.MESH
 
 
@@ -51,7 +52,8 @@
 
 
 def join(from_left, from_right, which):
-    return jnp.where(which < 2, pltpu.roll(from_right, LANES - 2, 1), pltpu.roll(from_left, 2, 1))
+    return (jnp.where(which < 2, pltpu.roll(from_right, LANES - 2, 1), pltpu.roll(from_left, 2, 1)),
+            jnp.where(which < 2, from_right, from_left))
 
 
 def exchange_kernel(dims, tracers, velocity, land_mask, sunlight, *refs):
@@ -60,12 +62,12 @@
     growth_max, half_sat, light_half, graze_max, graze_half, palatable, stoichiometry = tables
     (
         pad, mask_buf, sun_buf, swept, pack, left_in, right_in, qpad, halo_term, across_buf,
-        corner_out, meta_out, meta_in, prey, load_sems, main_sems, send_sems, recv_sems, ready_sems,
+        corner_out, shifts, meta_out, meta_in, prey, load_sems, main_sems, send_sems, recv_sems, ready_sems,
     ) = buffers
     count, levels, along, nphy, nzoo, stride = dims
     tiles = along // ROWS
     flow_field, wet_field, cross_field = count, count + 1, count + 2
-    groups = pack.shape[1]
+    groups = qpad.shape[1] - 2
     tx_size, ty_size = lax.axis_size("tx"), lax.axis_size("ty")
     tx, ty = lax.axis_index("tx"), lax.axis_index("ty")
     up, down = lax.rem(tx + 1, tx_size), lax.rem(tx + tx_size - 1, tx_size)
@@ -174,14 +176,14 @@
     up_meta = remote(META, meta_out.at[1], meta_in.at[0], tx=up)
     down_meta = remote(META, meta_out.at[0], meta_in.at[1], tx=down)
     to_right = [
-        remote(RIGHT_CORNERS, corner_out.at[1], corner_left.at[0], tx=up, ty=right),
-        remote(RIGHT_CORNERS, corner_out.at[0], corner_left.at[1], tx=down, ty=right),
-        remote(RIGHT_COLUMNS, pack, left_in, ty=right),
+        remote(RIGHT_CORNERS, corner_out.at[1, 1], corner_left.at[0], tx=up, ty=right),
+        remote(RIGHT_CORNERS, corner_out.at[1, 0], corner_left.at[1], tx=down, ty=right),
+        remote(RIGHT_COLUMNS, pack.at[1], left_in, ty=right),
     ]
     to_left = [
-        remote(LEFT_CORNERS, corner_out.at[1], corner_right.at[0], tx=up, ty=left),
-        remote(LEFT_CORNERS, corner_out.at[0], corner_right.at[1], tx=down, ty=left),
-        remote(LEFT_COLUMNS, pack, right_in, ty=left),
+        remote(LEFT_CORNERS, corner_out.at[0, 1], corner_right.at[0], tx=up, ty=left),
+        remote(LEFT_CORNERS, corner_out.at[0, 0], corner_right.at[1], tx=down, ty=left),
+        remote(LEFT_COLUMNS, pack.at[0], right_in, ty=left),
     ]
     both_rows = remote(ROW, far, far, tx=up)
     both_metas = remote(META, meta_in, meta_in, tx=up)
@@ -197,6 +199,11 @@
     def start_sides(edge):
         start(has_right, [to_right[1 - edge]])
         start(has_left, [to_left[1 - edge]])
+
+    source = lax.broadcasted_iota(jnp.int32, (2 * LANES, LANES), 0) % LANES
+    target = lax.broadcasted_iota(jnp.int32, (2 * LANES, LANES), 1)
+    for i, offset in enumerate((-2, -1, 1, 2)):
+        shifts[:, i * LANES:(i + 1) * LANES] = jnp.where(source == target + offset, 1.0, 0.0).astype(jnp.bfloat16)
 
     await_load(OWN_UP, own.at[1, :, pl.ds(2, 2)])
     odd_core = lax.rem(ty, 2) == 1
@@ -246,12 +253,14 @@
                         packed[group] = jnp.where(lane_group == place, turned, packed[group])
                 for field, value in zip(batch, values):
                     swept[field, level, tile * ROWS:(tile + 1) * ROWS, :] = value
-            for group, value in enumerate(packed):
-                pack[level, group, tile * ROWS:(tile + 1) * ROWS, :] = value
+            for_left = jnp.where(quarter >= 2, packed[0], pltpu.roll(packed[1], LANES - 2, 1))
+            for_right = jnp.where(quarter < 2, packed[0], pltpu.roll(packed[1], 2, 1))
+            for side, value in enumerate((for_left, for_right)):
+                pack[side, level, tile * ROWS:(tile + 1) * ROWS, :] = value
                 for edge, edge_tile, row in ((0, 0, 0), (1, tiles - 1, ROWS - 2)):
                     if tile == edge_tile:
                         for r in range(2):
-                            corner_out[edge, r, pl.ds(level * groups + group, 1), :] = value[row + r:row + r + 1, :]
+                            corner_out[side, edge, r, pl.ds(level, 1), :] = value[row + r:row + r + 1, :]
         return carry
 
     lax.fori_loop(0, levels, sweep_level, 0)
@@ -371,21 +380,28 @@
             to_left.wait_send()
             to_right.wait_recv()
 
+    @pl.when(at_first)
+    def _():
+        @pl.when(sides > 0)
+        def _():
+            pl.semaphore_wait(ready_sems.at[TO_DOWN_SIDES], sides)
+
+        start_sides(0)
+
     finish(to_right[2], to_left[2])
     full_lane = lax.broadcasted_iota(jnp.int32, (along, LANES), 1)
     full_quarter = full_lane % GROUP
     full = (along, LANES)
-    ends = jnp.logical_or(lane < 2, lane >= LANES - 2)
+    full_ends = jnp.logical_or(full_lane < 2, full_lane >= LANES - 2)
 
     def halo_level(level):
         middle = pl.ds(FIRST, along)
         joined = []
-        for group in range(groups):
-            value = join(left_in[level, group], right_in[level, group], full_quarter)
+        for group, value in enumerate(join(left_in[level], right_in[level], full_quarter)):
             qpad[level, group, middle, :] = value
             joined.append(value)
             for k in range(4):
-                spot = slice(level * groups + group, level * groups + group + 1)
+                spot = slice(group * HALF + level, group * HALF + level + 1)
                 strips[0, 2 + k, spot, :] = value[k:k + 1, :]
                 strips[1, k, spot, :] = value[along - 4 + k:along - 3 + k, :]
         last = joined[groups - 1]
@@ -427,7 +443,7 @@
                 for i, value in enumerate(masked):
                     across_w[edge, level, r, i:i + 1, :] = value[row + r:row + r + 1, :]
                 for group in range(groups):
-                    spot = slice(level * groups + group, level * groups + group + 1)
+                    spot = slice(group * HALF + level, group * HALF + level + 1)
                     halo_w[0, edge, r, spot, :] = near[row + r:row + r + 1, :]
                     halo_w[1, edge, r, spot, :] = next_to[row + r:row + r + 1, :]
         for group in range(groups):
@@ -441,31 +457,22 @@
         halo_level(level)
 
     def across_level(level, carry):
-        @pl.when(jnp.logical_and(at_first, level == min(1, levels - 1)))
-        def _():
-            @pl.when(sides > 0)
-            def _():
-                pl.semaphore_wait(ready_sems.at[TO_DOWN_SIDES], sides)
-
-            start_sides(0)
-
-        for tile in range(tiles):
-            rows = slice(tile * ROWS, (tile + 1) * ROWS)
-            w = [across_buf[level, i, rows, :] for i in range(5)]
-            terms = [halo_term[level, group, rows, :] for group in range(groups)]
-            for begin in range(0, count, BATCH):
-                batch = range(begin, min(begin + BATCH, count))
-                totals = []
-                for field in batch:
-                    group, place = place_of(field)
-                    value = swept[field, level, rows, :]
-                    total = tend[tend_rows(field, level, tile * ROWS, ROWS), :] + value * w[2]
-                    total = total + pltpu.roll(value, 2, 1) * w[0] + pltpu.roll(value, 1, 1) * w[1]
-                    total = total + pltpu.roll(value, LANES - 1, 1) * w[3] + pltpu.roll(value, LANES - 2, 1) * w[4]
-                    term = pltpu.roll(terms[group], (LANES - 2 - GROUP * place) % LANES, 1)
-                    totals.append(total + jnp.where(ends, term, 0.0))
-                for field, total in zip(batch, totals):
-                    result[field, level, rows, :] = total
+        w = [across_buf[level, i] for i in range(5)]
+        terms = [halo_term[level, group] for group in range(groups)]
+        for begin in range(0, count, BATCH):
+            batch = range(begin, min(begin + BATCH, count))
+            block = jnp.concatenate([swept[field, level] for field in batch], axis=0)
+            coarse = block.astype(jnp.bfloat16)
+            rest = (block - coarse.astype(jnp.float32)).astype(jnp.bfloat16)
+            near = jnp.dot(jnp.concatenate([coarse, rest], axis=1), shifts[...], preferred_element_type=jnp.float32)
+            for i, field in enumerate(batch):
+                group, place = place_of(field)
+                part = near[i * along:(i + 1) * along]
+                total = tend[tend_rows(field, level), :] + block[i * along:(i + 1) * along] * w[2]
+                for k, weight in enumerate((w[0], w[1], w[3], w[4])):
+                    total = total + part[:, k * LANES:(k + 1) * LANES] * weight
+                term = pltpu.roll(terms[group], (LANES - 2 - GROUP * place) % LANES, 1)
+                result[field, level] = total + jnp.where(full_ends, term, 0.0)
         return carry
 
     lax.fori_loop(0, levels, across_level, 0)
@@ -505,18 +512,17 @@
     lane = lax.broadcasted_iota(jnp.int32, (ROWS, LANES), 1)
     quarter = lane % GROUP
     ends = jnp.logical_or(lane < 2, lane >= LANES - 2)
-    odd = lax.broadcasted_iota(jnp.int32, (ROWS, LANES), 0) % groups == groups - 1
+    upper = lax.broadcasted_iota(jnp.int32, (ROWS, LANES), 0) >= HALF
 
     def both(value):
-        return jnp.where(odd, value, pltpu.roll(value, ROWS - 1, 0))
+        return jnp.where(upper, value, pltpu.roll(value, HALF, 0))
 
     terms = {}
     for edge in range(2):
-        strip = [
-            join(corner_left[edge, k - 4 * edge], corner_right[edge, k - 4 * edge], quarter)
-            if k - 4 * edge in (0, 1) else strips[edge, k]
-            for k in range(6)
-        ]
+        strip = [strips[edge, k] for k in range(6)]
+        for r in range(2):
+            first, second = join(corner_left[edge, r], corner_right[edge, r], quarter)
+            strip[r + 4 * edge] = jnp.where(upper, pltpu.roll(second, HALF, 0), first)
         wets = {k: both(packed_spread(strip[k], wet_field, quarter)) for k in range(1, 5)}
         flows = {k: both(packed_spread(strip[k], flow_field, quarter)) for k in range(2, 5)}
         faces = {k: flows[k] * wets[k - 1] * wets[k] for k in range(2, 5)}
@@ -546,7 +552,7 @@
                 total = total + pltpu.roll(value, LANES - 2, 1) * across_lines[4:5, :]
                 for begin in range(0, count, ROWS):
                     group, inside = divmod(begin, PER)
-                    spot = level * groups + group
+                    spot = group * HALF + level
                     line = jnp.broadcast_to(terms[edge, r][spot:spot + 1, :], (ROWS, LANES))
                     line = pltpu.roll(line, 2 + GROUP * inside, 1, stride=GROUP, stride_axis=0)
                     rows = pl.ds(begin * stride + level * along + row, ROWS, stride=stride)
@@ -575,7 +581,7 @@
     nphy, nzoo = growth_max.shape[0], graze_max.shape[0]
     groups = -(-(count + 3) // PER)
     assert across == LANES and along % ROWS == 0 and along >= 2 * ROWS
-    assert count % ROWS == 0 and groups == 2 and (count + 2) % PER >= 2 and levels * groups <= ROWS
+    assert count % ROWS == 0 and groups == 2 and (count + 2) % PER >= 2 and levels <= HALF
     f32 = jnp.float32
     any_space = pl.BlockSpec(memory_space=pl.ANY)
     hbm = pl.BlockSpec(memory_space=pltpu.HBM)
@@ -583,7 +589,7 @@
     small = (growth_max, half_sat, light_half, graze_max, graze_half, palatable, stoichiometry)
     stride = levels * along + ROWS
     line = (ROWS, LANES)
-    columns = (levels, groups, along, LANES)
+    columns = (levels, along, LANES)
     outputs = [
         (count, levels, along, LANES),
         (2, levels, 4, count, LANES),
@@ -606,13 +612,14 @@
             pltpu.VMEM(land_mask.shape, jnp.int32),
             pltpu.VMEM(sunlight.shape, f32),
             pltpu.VMEM((count, levels, along, LANES), f32),
-            pltpu.VMEM(columns, f32),
+            pltpu.VMEM((2,) + columns, f32),
             pltpu.VMEM(columns, f32),
             pltpu.VMEM(columns, f32),
             pltpu.VMEM((levels, groups + 2, FIRST + along + ROWS, LANES), f32),
             pltpu.VMEM((levels, groups, along, LANES), f32),
             pltpu.VMEM((levels, 5, along, LANES), f32),
-            pltpu.VMEM((2, 2) + line, f32),
+            pltpu.VMEM((2, 2, 2) + line, f32),
+            pltpu.VMEM((2 * LANES, 4 * LANES), jnp.bfloat16),
             pltpu.VMEM((2, 2, levels, 2, LANES), f32),
             pltpu.VMEM((2, 2, levels, 2, LANES), f32),
             pltpu.SMEM(palatable.shape, f32),

time: 13.2 us -> 13.4 us (1.015)
  Pallas kernels: 13 us -> 13.2 us
    pallas_call x1, Pallas kernels: 11.5 us -> 11.7 us  [shards(): pl.pallas_call(functools.partial(exchange_kernel, (count, levels, along,...]
where the time goes in v5:
time: 13.4 us; the launch traced here: 13.2 us
  Pallas kernels  13.2 us (99%)
    pallas_call x1, Pallas kernels, shards(): pl.pallas_call(functools.partial(exchange_kernel, (count, levels, along,...  11.7 us
    pallas_call x1, Pallas kernels, shards(): pl.pallas_call(functools.partial(across_kernel, (count, levels, along, st...  1.54 us

profile of v5, /device:TPU:1, one launch (start us, length us, event | category | flops | bytes accessed | tf_op | source)
XLA Modules:
  0.0 13.2 jit_solution(2672108894177638163)
XLA Ops:
  0.0 11.7 %exchange.1 = (f32[40,3,32,128]{3,2,1,0:T(8,128)S(1)}, f32[2,3,4,40,128]{4,3,2,1,0:T(8,128)S(1)}, f32[2,3,2,40,128]{4,3,2,1,0:T(8,128)S(1)}, f32[4160,128]{1,0:T...) custom-call(f32[40,3,32,128]{3,2,1,0:T(8,128)} %tracers.1, ...), custom_call_target="tpu_custom_call" | custom-call | tf_op jit(solution)/shard_map/exchange/pallas_call | solution.py:605
  11.7 1.5 %across.1 = f32[40,3,32,128]{3,2,1,0:T(8,128)} custom-call(f32[40,3,32,128]{3,2,1,0:T(8,128)S(1)} %get-tuple-element.15.result, f32[2,3,4,40,128]{4,3,2,1,0:T(8,128)S(1)} %get-tuple-element.16.own, f32[2,3,2,40,128]{4,3,2,1,0:T(8,128)S(1)} %get-tuple-element.17.far, f32[4160,128]{1,0:T(8,128)S(1)} %get-tuple-element.18.tend, ...), custom_call_target="tpu_custom_call" | custom-call | tf_op jit(solution)/shard_map/across/pallas_call | solution.py:640

commit v6 on v5

--- a/solution.py
+++ b/solution.py
@@ -171,8 +171,12 @@
             device_id=target, device_id_type=MESH)
 
     ROW, META, RIGHT_CORNERS, RIGHT_COLUMNS, LEFT_CORNERS, LEFT_COLUMNS = range(6)
-    up_rows = remote(ROW, own.at[1, :, pl.ds(2, 2)], far.at[0], tx=up)
-    down_rows = remote(ROW, own.at[0, :, pl.ds(0, 2)], far.at[1], tx=down)
+    up_pieces = [
+        remote(ROW, own.at[1, level, pl.ds(2, 2)], far.at[0, level], tx=up) for level in range(levels)
+    ]
+    down_pieces = [
+        remote(ROW, own.at[0, level, pl.ds(0, 2)], far.at[1, level], tx=down) for level in range(levels)
+    ]
     up_meta = remote(META, meta_out.at[1], meta_in.at[0], tx=up)
     down_meta = remote(META, meta_out.at[0], meta_in.at[1], tx=down)
     to_right = [
@@ -207,23 +211,43 @@
 
     await_load(OWN_UP, own.at[1, :, pl.ds(2, 2)])
     odd_core = lax.rem(ty, 2) == 1
-    start(jnp.logical_and(at_last, jnp.logical_not(odd_core)), [up_rows])
+    even_core = jnp.logical_not(odd_core)
+    start(jnp.logical_and(at_last, even_core), up_pieces)
     await_load(OWN_DOWN, own.at[0, :, pl.ds(0, 2)])
+    middle = jnp.logical_not(jnp.logical_or(at_first, at_last))
+    start(jnp.logical_and(middle, even_core), down_pieces)
     await_load(PLANES, pad.at[pl.ds(count, 3), :, pl.ds(FIRST, along), :])
     pad[wet_field, :, FIRST:FIRST + along, :] = mask_buf[...].astype(jnp.float32)
-    for edge, row in enumerate((FIRST, FIRST + along - 2)):
-        meta_out[edge, 0] = pad[flow_field, :, row:row + 2, :]
-        meta_out[edge, 1] = pad[wet_field, :, row:row + 2, :]
+    for edge, row in enumerate((FIRST, FIRST + along - 1)):
+        for i, field in enumerate((flow_field, wet_field)):
+            for level in range(levels):
+                meta_out[edge, i * HALF + level:i * HALF + level + 1, :] = pad[field, level, row:row + 1, :]
     start(at_last, [up_meta, down_meta])
-    middle = jnp.logical_not(jnp.logical_or(at_first, at_last))
-    start(middle, [down_meta, down_rows])
+    start(middle, [down_meta])
+    start(jnp.logical_and(middle, odd_core), down_pieces[:2])
 
     lane = lax.broadcasted_iota(jnp.int32, (ROWS, LANES), 1)
     lane_group = lane // GROUP
     quarter = lane % GROUP
 
+    upward = jnp.logical_and(others, jnp.logical_not(at_last))
+
+    beside_root = jnp.logical_and(at_first, jnp.logical_and(lax.axis_index("member") == 0, ty == 2))
+    eager = jnp.logical_and(jnp.logical_and(upward, even_core), jnp.logical_not(beside_root))
+
+    def send_up(pieces):
+        pl.semaphore_wait(ready_sems.at[TO_UP], 1)
+        up_meta.start()
+        for piece in pieces:
+            piece.start()
+
     def sweep_level(level, carry):
         main(level).wait()
+
+        @pl.when(jnp.logical_and(eager, level == min(1, levels - 1)))
+        def _():
+            send_up(up_pieces[:1])
+
 
         for tile in (0, tiles - 1, *range(1, tiles - 1)):
             start_row = FIRST + tile * ROWS
@@ -253,43 +277,55 @@
                         packed[group] = jnp.where(lane_group == place, turned, packed[group])
                 for field, value in zip(batch, values):
                     swept[field, level, tile * ROWS:(tile + 1) * ROWS, :] = value
-            for_left = jnp.where(quarter >= 2, packed[0], pltpu.roll(packed[1], LANES - 2, 1))
-            for_right = jnp.where(quarter < 2, packed[0], pltpu.roll(packed[1], 2, 1))
-            for side, value in enumerate((for_left, for_right)):
-                pack[side, level, tile * ROWS:(tile + 1) * ROWS, :] = value
-                for edge, edge_tile, row in ((0, 0, 0), (1, tiles - 1, ROWS - 2)):
-                    if tile == edge_tile:
-                        for r in range(2):
-                            corner_out[side, edge, r, pl.ds(level, 1), :] = value[row + r:row + r + 1, :]
+            for group, value in enumerate(packed):
+                qpad[level, group, tile * ROWS:(tile + 1) * ROWS, :] = value
         return carry
 
     lax.fori_loop(0, levels, sweep_level, 0)
+    full_lane = lax.broadcasted_iota(jnp.int32, (along, LANES), 1)
+    full_quarter = full_lane % GROUP
+    for level in range(levels):
+        one, two = (qpad[level, group, 0:along, :] for group in range(groups))
+        for_left = jnp.where(full_quarter >= 2, one, pltpu.roll(two, LANES - 2, 1))
+        for_right = jnp.where(full_quarter < 2, one, pltpu.roll(two, 2, 1))
+        for side, value in enumerate((for_left, for_right)):
+            pack[side, level] = value
+            for edge, row in ((0, 0), (1, along - 2)):
+                for r in range(2):
+                    corner_out[side, edge, r * HALF + level:r * HALF + level + 1, :] = value[row + r:row + r + 1, :]
     for copy in small:
         copy.wait()
     sun.wait()
 
-    def send_up():
-        pl.semaphore_wait(ready_sems.at[TO_UP], 1)
-        up_meta.start()
-        up_rows.start()
-
-    def send_down():
-        pl.semaphore_wait(ready_sems.at[TO_DOWN], 1)
-        down_meta.start()
-        down_rows.start()
-
+    pl.when(jnp.logical_not(at_first))(lambda: start_sides(0))
     pl.when(at_last)(lambda: start_sides(1))
-    pl.when(jnp.logical_not(at_first))(lambda: start_sides(0))
     start(has_left, [to_left[2]])
-    start(jnp.logical_and(at_last, odd_core), [up_rows])
-    start(at_last, [down_rows])
-    pl.when(jnp.logical_and(others, jnp.logical_not(at_last)))(send_up)
+
+    def send_up_sides():
+        @pl.when(sides > 0)
+        def _():
+            pl.semaphore_wait(ready_sems.at[TO_UP_SIDES], sides)
+
+        start_sides(1)
+
+    def send_down_sides():
+        @pl.when(sides > 0)
+        def _():
+            pl.semaphore_wait(ready_sems.at[TO_DOWN_SIDES], sides)
+
+        start_sides(0)
+
+    pl.when(upward)(send_up_sides)
 
     @pl.when(has_right)
     def _():
         pl.semaphore_wait(ready_sems.at[TO_RIGHT], 1)
         to_right[2].start()
 
+    start(jnp.logical_and(at_last, odd_core), up_pieces)
+    start(jnp.logical_and(middle, odd_core), down_pieces[2:])
+    start(eager, up_pieces[1:])
+    pl.when(jnp.logical_and(upward, jnp.logical_not(eager)))(lambda: send_up(up_pieces))
 
     for z in range(nzoo):
         for k in range(nphy):
@@ -299,17 +335,38 @@
         return pl.ds(pl.multiple_of(field * stride + level * along + row, ROWS), size)
 
     def ecology(level, carry):
-        second = level == min(1, levels - 1)
-        pl.when(jnp.logical_and(root, second))(send_up)
-        pl.when(jnp.logical_and(jnp.logical_and(at_first, others), second))(send_down)
-
-        @pl.when(jnp.logical_and(jnp.logical_not(at_last), second))
-        def _():
-            @pl.when(sides > 0)
-            def _():
-                pl.semaphore_wait(ready_sems.at[TO_UP_SIDES], sides)
-
-            start_sides(1)
+        second, third = level == min(1, levels - 1), level == levels - 1
+
+        @pl.when(jnp.logical_and(jnp.logical_and(root, even_core), level == 0))
+        def _():
+            send_up(up_pieces)
+
+        pl.when(jnp.logical_and(root, second))(send_up_sides)
+
+        @pl.when(jnp.logical_and(jnp.logical_and(root, odd_core), second))
+        def _():
+            send_up(up_pieces)
+
+        @pl.when(jnp.logical_and(root, third))
+        def _():
+            pl.semaphore_wait(ready_sems.at[TO_DOWN], 1)
+            down_meta.start()
+            for piece in down_pieces:
+                piece.start()
+
+        start(jnp.logical_and(at_last, second), down_pieces)
+
+        @pl.when(jnp.logical_and(jnp.logical_and(at_first, others), second))
+        def _():
+            pl.semaphore_wait(ready_sems.at[TO_DOWN], 1)
+            down_meta.start()
+            down_pieces[0].start()
+
+        @pl.when(jnp.logical_and(jnp.logical_and(at_first, others), third))
+        def _():
+            send_down_sides()
+            for piece in down_pieces[1:]:
+                piece.start()
 
         def field(index):
             return pad[index, level, pl.ds(FIRST, along), :]
@@ -356,8 +413,8 @@
         return carry
 
     lax.fori_loop(0, levels, ecology, 0)
-    pl.when(root)(send_down)
-
+
+    pl.when(root)(send_down_sides)
 
     @pl.when(jnp.logical_not(has_left))
     def _():
@@ -380,17 +437,7 @@
             to_left.wait_send()
             to_right.wait_recv()
 
-    @pl.when(at_first)
-    def _():
-        @pl.when(sides > 0)
-        def _():
-            pl.semaphore_wait(ready_sems.at[TO_DOWN_SIDES], sides)
-
-        start_sides(0)
-
     finish(to_right[2], to_left[2])
-    full_lane = lax.broadcasted_iota(jnp.int32, (along, LANES), 1)
-    full_quarter = full_lane % GROUP
     full = (along, LANES)
     full_ends = jnp.logical_or(full_lane < 2, full_lane >= LANES - 2)
 
@@ -479,9 +526,10 @@
 
     await_load(OWN_KEPT, far)
     both_metas.wait()
-    pad[wet_field, :, FIRST - 2:FIRST, :] = meta_in[0, 1]
-    for i, index in enumerate((flow_field, wet_field)):
-        pad[index, :, FIRST + along:FIRST + along + 2, :] = meta_in[1, i]
+    for level in range(levels):
+        pad[wet_field, level, FIRST - 1:FIRST, :] = meta_in[0, HALF + level:HALF + level + 1, :]
+        for i, index in enumerate((flow_field, wet_field)):
+            pad[index, level, FIRST + along:FIRST + along + 1, :] = meta_in[1, i * HALF + level:i * HALF + level + 1, :]
     for level in range(levels):
         for edge, tile, row in ((0, 0, 0), (1, tiles - 1, ROWS - 2)):
             start = FIRST + tile * ROWS
@@ -520,9 +568,9 @@
     terms = {}
     for edge in range(2):
         strip = [strips[edge, k] for k in range(6)]
-        for r in range(2):
-            first, second = join(corner_left[edge, r], corner_right[edge, r], quarter)
-            strip[r + 4 * edge] = jnp.where(upper, pltpu.roll(second, HALF, 0), first)
+        first, second = join(corner_left[edge], corner_right[edge], quarter)
+        strip[4 * edge] = jnp.where(upper, pltpu.roll(second, HALF, 0), first)
+        strip[4 * edge + 1] = jnp.where(upper, second, pltpu.roll(first, HALF, 0))
         wets = {k: both(packed_spread(strip[k], wet_field, quarter)) for k in range(1, 5)}
         flows = {k: both(packed_spread(strip[k], flow_field, quarter)) for k in range(2, 5)}
         faces = {k: flows[k] * wets[k - 1] * wets[k] for k in range(2, 5)}
@@ -598,8 +646,8 @@
         (2, levels, 2) + line,
         (2, levels, 2) + line,
         (2, 6) + line,
-        (2, 2) + line,
-        (2, 2) + line,
+        (2,) + line,
+        (2,) + line,
         (2, 2, 2) + line,
     ]
     prepared = pl.pallas_call(
@@ -618,10 +666,10 @@
             pltpu.VMEM((levels, groups + 2, FIRST + along + ROWS, LANES), f32),
             pltpu.VMEM((levels, groups, along, LANES), f32),
             pltpu.VMEM((levels, 5, along, LANES), f32),
-            pltpu.VMEM((2, 2, 2) + line, f32),
+            pltpu.VMEM((2, 2) + line, f32),
             pltpu.VMEM((2 * LANES, 4 * LANES), jnp.bfloat16),
-            pltpu.VMEM((2, 2, levels, 2, LANES), f32),
-            pltpu.VMEM((2, 2, levels, 2, LANES), f32),
+            pltpu.VMEM((2,) + line, f32),
+            pltpu.VMEM((2,) + line, f32),
             pltpu.SMEM(palatable.shape, f32),
             pltpu.SemaphoreType.DMA((8,)),
             pltpu.SemaphoreType.DMA((levels,)),

time: 13.4 us -> 12.8 us (0.955)
  the two profiles are of different devices: /device:TPU:1 before, /device:TPU:0 now
where the time goes in v6:
time: 12.8 us; the launch traced here: 12.6 us
  Pallas kernels  12.6 us (98%)
    pallas_call x1, Pallas kernels, shards(): pl.pallas_call(functools.partial(exchange_kernel, (count, levels, along,...  11.4 us
    pallas_call x1, Pallas kernels, shards(): pl.pallas_call(functools.partial(across_kernel, (count, levels, along, st...  1.27 us

profile of v6, /device:TPU:0, one launch (start us, length us, event | category | flops | bytes accessed | tf_op | source)
XLA Modules:
  0.0 12.6 jit_solution(1521658227118985094)
XLA Ops:
  0.0 11.4 %exchange.1 = (f32[40,3,32,128]{3,2,1,0:T(8,128)S(1)}, f32[2,3,4,40,128]{4,3,2,1,0:T(8,128)S(1)}, f32[2,3,2,40,128]{4,3,2,1,0:T(8,128)S(1)}, f32[4160,128]{1,0:T...) custom-call(f32[40,3,32,128]{3,2,1,0:T(8,128)} %tracers.1, ...), custom_call_target="tpu_custom_call" | custom-call | tf_op jit(solution)/shard_map/exchange/pallas_call | solution.py:653
  11.4 1.3 %across.1 = f32[40,3,32,128]{3,2,1,0:T(8,128)} custom-call(f32[40,3,32,128]{3,2,1,0:T(8,128)S(1)} %get-tuple-element.15.result, f32[2,3,4,40,128]{4,3,2,1,0:T(8,128)S(1)} %get-tuple-element.16.own, f32[2,3,2,40,128]{4,3,2,1,0:T(8,128)S(1)} %get-tuple-element.17.far, f32[4160,128]{1,0:T(8,128)S(1)} %get-tuple-element.18.tend, ...), custom_call_target="tpu_custom_call" | custom-call | tf_op jit(solution)/shard_map/across/pallas_call | solution.py:688

commit v7 on v6

--- a/solution.py
+++ b/solution.py
@@ -57,11 +57,11 @@
 
 
 def exchange_kernel(dims, tracers, velocity, land_mask, sunlight, *refs):
-    sources, outs, tables, buffers = refs[:7], refs[7:17], refs[17:24], refs[24:]
-    result, own, far, tend, along_w, across_w, strips, corner_left, corner_right, halo_w = outs
+    sources, outs, tables, buffers = refs[:7], refs[7:13], refs[13:20], refs[20:]
+    result, own, far, base, along_w, across_w = outs
     growth_max, half_sat, light_half, graze_max, graze_half, palatable, stoichiometry = tables
     (
-        pad, mask_buf, sun_buf, swept, pack, left_in, right_in, qpad, halo_term, across_buf,
+        pad, mask_buf, sun_buf, swept, tend, strips, corner_left, corner_right, halo_w, pack, left_in, right_in, qpad, halo_term, across_buf,
         corner_out, shifts, meta_out, meta_in, prey, load_sems, main_sems, send_sems, recv_sems, ready_sems,
     ) = buffers
     count, levels, along, nphy, nzoo, stride = dims
@@ -215,7 +215,7 @@
     start(jnp.logical_and(at_last, even_core), up_pieces)
     await_load(OWN_DOWN, own.at[0, :, pl.ds(0, 2)])
     middle = jnp.logical_not(jnp.logical_or(at_first, at_last))
-    start(jnp.logical_and(middle, even_core), down_pieces)
+    start(jnp.logical_and(middle, even_core), down_pieces[:2])
     await_load(PLANES, pad.at[pl.ds(count, 3), :, pl.ds(FIRST, along), :])
     pad[wet_field, :, FIRST:FIRST + along, :] = mask_buf[...].astype(jnp.float32)
     for edge, row in enumerate((FIRST, FIRST + along - 1)):
@@ -299,6 +299,7 @@
 
     pl.when(jnp.logical_not(at_first))(lambda: start_sides(0))
     pl.when(at_last)(lambda: start_sides(1))
+    start(middle, down_pieces[2:])
     start(has_left, [to_left[2]])
 
     def send_up_sides():
@@ -323,7 +324,6 @@
         to_right[2].start()
 
     start(jnp.logical_and(at_last, odd_core), up_pieces)
-    start(jnp.logical_and(middle, odd_core), down_pieces[2:])
     start(eager, up_pieces[1:])
     pl.when(jnp.logical_and(upward, jnp.logical_not(eager)))(lambda: send_up(up_pieces))
 
@@ -545,20 +545,6 @@
                     along_w[edge, level, r, i:i + 1, :] = value[row + r:row + r + 1, :]
 
     finish(right_corners, left_corners)
-    both_rows.wait()
-
-
-def across_kernel(dims, result, own, far, tend, along_w, across_w, strips, corner_left, corner_right, halo_w,
-                  updated, rows_out, sems):
-    count, levels, along, stride = dims
-    groups = -(-(count + 3) // PER)
-    flow_field, wet_field = count, count + 1
-    inner = pl.ds(2, along - 4)
-    whole = pltpu.make_async_copy(result.at[:, :, inner, :], updated.at[:, :, inner, :], sems.at[0])
-    whole.start()
-
-    lane = lax.broadcasted_iota(jnp.int32, (ROWS, LANES), 1)
-    quarter = lane % GROUP
     ends = jnp.logical_or(lane < 2, lane >= LANES - 2)
     upper = lax.broadcasted_iota(jnp.int32, (ROWS, LANES), 0) >= HALF
 
@@ -584,6 +570,27 @@
 
     for edge in range(2):
         for level in range(levels):
+            for r in range(2):
+                row = r if edge == 0 else along - 2 + r
+                for begin in range(0, count, ROWS):
+                    group, inside = divmod(begin, PER)
+                    spot = group * HALF + level
+                    line = jnp.broadcast_to(terms[edge, r][spot:spot + 1, :], (ROWS, LANES))
+                    line = pltpu.roll(line, 2 + GROUP * inside, 1, stride=GROUP, stride_axis=0)
+                    rows = pl.ds(begin * stride + level * along + row, ROWS, stride=stride)
+                    base[edge, level, r, begin:begin + ROWS, :] = tend[rows, :] + jnp.where(ends, line, 0.0)
+
+    both_rows.wait()
+
+
+def across_kernel(dims, result, own, far, base, along_w, across_w, updated, rows_out, sems):
+    count, levels, along = dims
+    inner = pl.ds(2, along - 4)
+    whole = pltpu.make_async_copy(result.at[:, :, inner, :], updated.at[:, :, inner, :], sems.at[0])
+    whole.start()
+
+    for edge in range(2):
+        for level in range(levels):
             near = [own[edge, level, k] for k in range(4)]
             beyond = [far[edge, level, k] for k in range(2)]
             lines = beyond + near if edge == 0 else near + beyond
@@ -593,19 +600,12 @@
                 value = lines[r] * along_lines[0:1, :]
                 for shift in range(1, 5):
                     value = value + lines[r + shift] * along_lines[shift:shift + 1, :]
-                total = value * across_lines[2:3, :]
+                total = base[edge, level, r] + value * across_lines[2:3, :]
                 total = total + pltpu.roll(value, 2, 1) * across_lines[0:1, :]
                 total = total + pltpu.roll(value, 1, 1) * across_lines[1:2, :]
                 total = total + pltpu.roll(value, LANES - 1, 1) * across_lines[3:4, :]
                 total = total + pltpu.roll(value, LANES - 2, 1) * across_lines[4:5, :]
-                for begin in range(0, count, ROWS):
-                    group, inside = divmod(begin, PER)
-                    spot = group * HALF + level
-                    line = jnp.broadcast_to(terms[edge, r][spot:spot + 1, :], (ROWS, LANES))
-                    line = pltpu.roll(line, 2 + GROUP * inside, 1, stride=GROUP, stride_axis=0)
-                    rows = pl.ds(begin * stride + level * along + row, ROWS, stride=stride)
-                    rows_out[edge, level, r, begin:begin + ROWS, :] = (
-                        total[begin:begin + ROWS, :] + tend[rows, :] + jnp.where(ends, line, 0.0))
+                rows_out[edge, level, r] = total
                 pltpu.make_async_copy(
                     rows_out.at[edge, level, r], updated.at[:, level, row, :], sems.at[1]).start()
     whole.wait()
@@ -642,13 +642,9 @@
         (count, levels, along, LANES),
         (2, levels, 4, count, LANES),
         (2, levels, 2, count, LANES),
-        (count * stride, LANES),
+        (2, levels, 2, count, LANES),
         (2, levels, 2) + line,
         (2, levels, 2) + line,
-        (2, 6) + line,
-        (2,) + line,
-        (2,) + line,
-        (2, 2, 2) + line,
     ]
     prepared = pl.pallas_call(
         functools.partial(exchange_kernel, (count, levels, along, nphy, nzoo, stride)),
@@ -660,6 +656,11 @@
             pltpu.VMEM(land_mask.shape, jnp.int32),
             pltpu.VMEM(sunlight.shape, f32),
             pltpu.VMEM((count, levels, along, LANES), f32),
+            pltpu.VMEM((count * stride, LANES), f32),
+            pltpu.VMEM((2, 6) + line, f32),
+            pltpu.VMEM((2,) + line, f32),
+            pltpu.VMEM((2,) + line, f32),
+            pltpu.VMEM((2, 2, 2) + line, f32),
             pltpu.VMEM((2,) + columns, f32),
             pltpu.VMEM(columns, f32),
             pltpu.VMEM(columns, f32),
@@ -686,7 +687,7 @@
         for x in (tracers, velocity, land_mask, sunlight) + small
     ])
     return pl.pallas_call(
-        functools.partial(across_kernel, (count, levels, along, stride)),
+        functools.partial(across_kernel, (count, levels, along)),
         out_shape=jax.ShapeDtypeStruct(tracers.shape, f32),
         in_specs=[vmem] * len(outputs),
         out_specs=any_space,

time: 12.8 us -> 12.8 us (level)
  no operation moved by 1% of the time
where the time goes in v7:
time: 12.8 us; the launch traced here: 12.7 us
  Pallas kernels  12.7 us (99%)
    pallas_call x1, Pallas kernels, shards(): pl.pallas_call(functools.partial(exchange_kernel, (count, levels, along,...  11.4 us
    pallas_call x1, Pallas kernels, shards(): pl.pallas_call(functools.partial(across_kernel, (count, levels, along)),...  1.27 us

profile of v7, /device:TPU:0, one launch (start us, length us, event | category | flops | bytes accessed | tf_op | source)
XLA Modules:
  0.0 12.7 jit_solution(10514554686855395411)
XLA Ops:
  0.0 11.4 %exchange.1 = (f32[40,3,32,128]{3,2,1,0:T(8,128)S(1)}, f32[2,3,4,40,128]{4,3,2,1,0:T(8,128)S(1)}, f32[2,3,2,40,128]{4,3,2,1,0:T(8,128)S(1)}, f32[2,3,2,40,128]{4...) custom-call(f32[40,3,32,128]{3,2,1,0:T(8,128)} %tracers.1, ...), custom_call_target="tpu_custom_call" | custom-call | tf_op jit(solution)/shard_map/exchange/pallas_call | solution.py:649
  11.4 1.3 %across.1 = f32[40,3,32,128]{3,2,1,0:T(8,128)} custom-call(f32[40,3,32,128]{3,2,1,0:T(8,128)S(1)} %get-tuple-element.11.result, f32[2,3,4,40,128]{4,3,2,1,0:T(8,128)S(1)} %get-tuple-element.12.own, f32[2,3,2,40,128]{4,3,2,1,0:T(8,128)S(1)} %get-tuple-element.13.far, f32[2,3,2,40,128]{4,3,2,1,0:T(8,128)S(1)} %get-tuple-element.14.base, ...), custom_call_target="tpu_custom_call" | custom-call | tf_op jit(solution)/shard_map/across/pallas_call | solution.py:689

commit v8 on v7

--- a/solution.py
+++ b/solution.py
@@ -215,7 +215,7 @@
     start(jnp.logical_and(at_last, even_core), up_pieces)
     await_load(OWN_DOWN, own.at[0, :, pl.ds(0, 2)])
     middle = jnp.logical_not(jnp.logical_or(at_first, at_last))
-    start(jnp.logical_and(middle, even_core), down_pieces[:2])
+    start(jnp.logical_and(middle, even_core), down_pieces)
     await_load(PLANES, pad.at[pl.ds(count, 3), :, pl.ds(FIRST, along), :])
     pad[wet_field, :, FIRST:FIRST + along, :] = mask_buf[...].astype(jnp.float32)
     for edge, row in enumerate((FIRST, FIRST + along - 1)):
@@ -224,7 +224,6 @@
                 meta_out[edge, i * HALF + level:i * HALF + level + 1, :] = pad[field, level, row:row + 1, :]
     start(at_last, [up_meta, down_meta])
     start(middle, [down_meta])
-    start(jnp.logical_and(middle, odd_core), down_pieces[:2])
 
     lane = lax.broadcasted_iota(jnp.int32, (ROWS, LANES), 1)
     lane_group = lane // GROUP
@@ -299,7 +298,6 @@
 
     pl.when(jnp.logical_not(at_first))(lambda: start_sides(0))
     pl.when(at_last)(lambda: start_sides(1))
-    start(middle, down_pieces[2:])
     start(has_left, [to_left[2]])
 
     def send_up_sides():
@@ -354,7 +352,7 @@
             for piece in down_pieces:
                 piece.start()
 
-        start(jnp.logical_and(at_last, second), down_pieces)
+        start(jnp.logical_or(jnp.logical_and(at_last, second), jnp.logical_and(jnp.logical_and(middle, odd_core), level == 0)), down_pieces)
 
         @pl.when(jnp.logical_and(jnp.logical_and(at_first, others), second))
         def _():

time: 12.8 us -> 12.2 us (0.953)
  the two profiles are of different devices: /device:TPU:0 before, /device:TPU:1 now
where the time goes in v8:
time: 12.2 us; the launch traced here: 12.1 us
  Pallas kernels  12.1 us (99%)
    pallas_call x1, Pallas kernels, shards(): pl.pallas_call(functools.partial(exchange_kernel, (count, levels, along,...  10.8 us
    pallas_call x1, Pallas kernels, shards(): pl.pallas_call(functools.partial(across_kernel, (count, levels, along)),...  1.27 us

profile of v8, /device:TPU:1, one launch (start us, length us, event | category | flops | bytes accessed | tf_op | source)
XLA Modules:
  0.0 12.1 jit_solution(2749328382730871243)
XLA Ops:
  0.0 10.8 %exchange.1 = (f32[40,3,32,128]{3,2,1,0:T(8,128)S(1)}, f32[2,3,4,40,128]{4,3,2,1,0:T(8,128)S(1)}, f32[2,3,2,40,128]{4,3,2,1,0:T(8,128)S(1)}, f32[2,3,2,40,128]{4...) custom-call(f32[40,3,32,128]{3,2,1,0:T(8,128)} %tracers.1, ...), custom_call_target="tpu_custom_call" | custom-call | tf_op jit(solution)/shard_map/exchange/pallas_call | solution.py:647
  10.8 1.3 %across.1 = f32[40,3,32,128]{3,2,1,0:T(8,128)} custom-call(f32[40,3,32,128]{3,2,1,0:T(8,128)S(1)} %get-tuple-element.11.result, f32[2,3,4,40,128]{4,3,2,1,0:T(8,128)S(1)} %get-tuple-element.12.own, f32[2,3,2,40,128]{4,3,2,1,0:T(8,128)S(1)} %get-tuple-element.13.far, f32[2,3,2,40,128]{4,3,2,1,0:T(8,128)S(1)} %get-tuple-element.14.base, ...), custom_call_target="tpu_custom_call" | custom-call | tf_op jit(solution)/shard_map/across/pallas_call | solution.py:687

commit v9 on v8

--- a/solution.py
+++ b/solution.py
@@ -215,7 +215,6 @@
     start(jnp.logical_and(at_last, even_core), up_pieces)
     await_load(OWN_DOWN, own.at[0, :, pl.ds(0, 2)])
     middle = jnp.logical_not(jnp.logical_or(at_first, at_last))
-    start(jnp.logical_and(middle, even_core), down_pieces)
     await_load(PLANES, pad.at[pl.ds(count, 3), :, pl.ds(FIRST, along), :])
     pad[wet_field, :, FIRST:FIRST + along, :] = mask_buf[...].astype(jnp.float32)
     for edge, row in enumerate((FIRST, FIRST + along - 1)):
@@ -224,6 +223,8 @@
                 meta_out[edge, i * HALF + level:i * HALF + level + 1, :] = pad[field, level, row:row + 1, :]
     start(at_last, [up_meta, down_meta])
     start(middle, [down_meta])
+    start(jnp.logical_and(middle, even_core), down_pieces)
+    start(jnp.logical_and(middle, odd_core), down_pieces[:1])
 
     lane = lax.broadcasted_iota(jnp.int32, (ROWS, LANES), 1)
     lane_group = lane // GROUP
@@ -352,7 +353,8 @@
             for piece in down_pieces:
                 piece.start()
 
-        start(jnp.logical_or(jnp.logical_and(at_last, second), jnp.logical_and(jnp.logical_and(middle, odd_core), level == 0)), down_pieces)
+        start(jnp.logical_and(at_last, second), down_pieces)
+        start(jnp.logical_and(jnp.logical_and(middle, odd_core), level == 0), down_pieces[1:])
 
         @pl.when(jnp.logical_and(jnp.logical_and(at_first, others), second))
         def _():

time: 12.2 us -> 12.8 us (1.049)
  Pallas kernels: 12.1 us -> 12.6 us
    pallas_call x1, Pallas kernels: 10.8 us -> 11.3 us  [shards(): pl.pallas_call(functools.partial(exchange_kernel, (count, levels, along,...]
where the time goes in v9:
time: 12.8 us; the launch traced here: 12.6 us
  Pallas kernels  12.6 us (98%)
    pallas_call x1, Pallas kernels, shards(): pl.pallas_call(functools.partial(exchange_kernel, (count, levels, along,...  11.3 us
    pallas_call x1, Pallas kernels, shards(): pl.pallas_call(functools.partial(across_kernel, (count, levels, along)),...  1.27 us

profile of v9, /device:TPU:1, one launch (start us, length us, event | category | flops | bytes accessed | tf_op | source)
XLA Modules:
  0.0 12.6 jit_solution(6980313175317439960)
XLA Ops:
  0.0 11.3 %exchange.1 = (f32[40,3,32,128]{3,2,1,0:T(8,128)S(1)}, f32[2,3,4,40,128]{4,3,2,1,0:T(8,128)S(1)}, f32[2,3,2,40,128]{4,3,2,1,0:T(8,128)S(1)}, f32[2,3,2,40,128]{4...) custom-call(f32[40,3,32,128]{3,2,1,0:T(8,128)} %tracers.1, ...), custom_call_target="tpu_custom_call" | custom-call | tf_op jit(solution)/shard_map/exchange/pallas_call | solution.py:649
  11.4 1.3 %across.1 = f32[40,3,32,128]{3,2,1,0:T(8,128)} custom-call(f32[40,3,32,128]{3,2,1,0:T(8,128)S(1)} %get-tuple-element.11.result, f32[2,3,4,40,128]{4,3,2,1,0:T(8,128)S(1)} %get-tuple-element.12.own, f32[2,3,2,40,128]{4,3,2,1,0:T(8,128)S(1)} %get-tuple-element.13.far, f32[2,3,2,40,128]{4,3,2,1,0:T(8,128)S(1)} %get-tuple-element.14.base, ...), custom_call_target="tpu_custom_call" | custom-call | tf_op jit(solution)/shard_map/across/pallas_call | solution.py:689
